TPU v7x, 256 devices: a whole 4x4x8 slice. The times are simulated.
256 devices in a mesh: gx: 4 (over x), gy: 8 (over z), gz: 8 (over y, core).
Axes of the slice: x: 4, y: 4, z: 8, core: 2. Of those that a mesh axis runs over, the one named last changes fastest.
Arguments:
- viscosity: float32 [128, 128, 1024], P('gx', 'gy', 'gz'), may hold values from 0.001 to 1000
- force: float32 [3, 128, 128, 1024], P(None, 'gx', 'gy', 'gz'), may hold values from -6 to 6
Outputs:
- solution: float32 [4, 128, 128, 1024], P(None, 'gx', 'gy', 'gz')
- residual: float32 [4, 128, 128, 1024], P(None, 'gx', 'gy', 'gz')
All inputs are finite; a program needn't handle non-finite values.
Results may differ from a plain program's by a relative error of at most 0.0003.
Values sent between devices are 32-bit elements; how exact they have to be, the bound alone decides.
No kernel may reach another device: no remote copies, remote signals or barrier semaphores. Data moves between devices by JAX's collectives and lax.ppermute only.
A program may use at most 128 MiB of HBM per device.

v0:
```python
import jax
import jax.numpy as jnp
from jax import lax
from jax.sharding import Mesh
from jax.sharding import PartitionSpec as P

CHEB = 4
ITERS = 2
GX_GY_GZ = ("gx", "gy", "gz_0", "gz_1")
GZ = ("gz_0", "gz_1")


low_edge = 0.25
high_edge = 2.0


def extended(cells, sides, width):
    for axis, dim in sides:
        count = lax.axis_size(axis)
        ends = count - 1
        head = lax.slice_in_dim(cells, 0, width, axis=dim)
        tail = lax.slice_in_dim(cells, cells.shape[dim] - width, cells.shape[dim], axis=dim)
        cells = jnp.concatenate(
            [
                lax.ppermute(tail, axis, [(i, (i + 1) % count) for i in range(ends)]),
                cells,
                lax.ppermute(head, axis, [((i + 1) % count, i) for i in range(ends)]),
            ],
            axis=dim,
        )
    return cells


def one_axis_at_a_time(shard, axes):
    for axis in axes:
        shard = lax.psum(shard, axis)
    return shard


def with_halo(shard, sides, width):
    edges = {}
    for axis, dim in sides:
        size, length = (lax.axis_size(axis), shard.shape[dim])
        up = [(i, (i + 1) % size) for i in range(size - 1)]
        last = lax.slice_in_dim(shard, length - width, length, axis=dim)
        initial = lax.slice_in_dim(shard, 0, width, axis=dim)
        edges[dim] = (
            lax.ppermute(last, axis, up),
            lax.ppermute(initial, axis, [(b, a) for a, b in up]),
        )
    done = []
    for _, dim in sides:
        low, high = edges[dim]
        around = [(width, width) if d in done else (0, 0) for d in range(shard.ndim)]
        shard = jnp.concatenate([jnp.pad(low, around), shard, jnp.pad(high, around)], axis=dim)
        done.append(dim)
    return shard


def coefficients(padded_eta):
    middle = padded_eta[1:-1, 1:-1, 1:-1]
    x_plus = 0.5 * (middle + padded_eta[2:, 1:-1, 1:-1])
    x_minus = 0.5 * (middle + padded_eta[:-2, 1:-1, 1:-1])
    y_plus = 0.5 * (middle + padded_eta[1:-1, 2:, 1:-1])
    y_minus = 0.5 * (middle + padded_eta[1:-1, :-2, 1:-1])
    z_plus = 0.5 * (middle + padded_eta[1:-1, 1:-1, 2:])
    z_minus = 0.5 * (middle + padded_eta[1:-1, 1:-1, :-2])
    diagonal = x_plus + x_minus + y_plus + y_minus + z_plus + z_minus
    return (x_plus, x_minus, y_plus, y_minus, z_plus, z_minus, diagonal)


def viscous(padded, stencil):
    x_plus, x_minus, y_plus, y_minus, z_plus, z_minus, diagonal = stencil
    result = diagonal * padded[:, 1:-1, 1:-1, 1:-1]
    result = result - x_plus * padded[:, 2:, 1:-1, 1:-1] - x_minus * padded[:, :-2, 1:-1, 1:-1]
    result = result - y_plus * padded[:, 1:-1, 2:, 1:-1] - y_minus * padded[:, 1:-1, :-2, 1:-1]
    result = result - z_plus * padded[:, 1:-1, 1:-1, 2:] - z_minus * padded[:, 1:-1, 1:-1, :-2]
    return result


def stokes(padded, stencil):
    velocity = padded[:3]
    pressure = padded[3]
    gradient = jnp.stack(
        [
            0.5 * (pressure[2:, 1:-1, 1:-1] - pressure[:-2, 1:-1, 1:-1]),
            0.5 * (pressure[1:-1, 2:, 1:-1] - pressure[1:-1, :-2, 1:-1]),
            0.5 * (pressure[1:-1, 1:-1, 2:] - pressure[1:-1, 1:-1, :-2]),
        ]
    )
    divergence = -0.5 * (
        velocity[0, 2:, 1:-1, 1:-1]
        - velocity[0, :-2, 1:-1, 1:-1]
        + (velocity[1, 1:-1, 2:, 1:-1] - velocity[1, 1:-1, :-2, 1:-1])
        + (velocity[2, 1:-1, 1:-1, 2:] - velocity[2, 1:-1, 1:-1, :-2])
    )
    return jnp.concatenate([viscous(velocity, stencil) + gradient, divergence[None]], axis=0)


def pad_cells(field):
    return jnp.pad(field, ((0, 0), (1, 1), (1, 1), (1, 1)))


def chebyshev(forcing, inverse, apply_block):
    middle = 0.5 * (high_edge + low_edge)
    half_width = 0.5 * (high_edge - low_edge)
    scaled = middle / half_width
    ratio_now = 1.0 / scaled
    update = forcing * inverse / middle
    result = update
    remainder = forcing
    for sweep_at in range(CHEB - 1):
        remainder = remainder - apply_block(update)
        ratio_next = 1.0 / (2.0 * scaled - ratio_now)
        update = (
            ratio_next * ratio_now * update + 2.0 * ratio_next / half_width * remainder * inverse
        )
        result = result + update
        ratio_now = ratio_next
    return result


def least_squares(columns, initial_norm):
    hessen = jnp.stack(columns, axis=1)
    normal = jnp.dot(hessen.T, hessen, precision=lax.Precision.HIGHEST)
    target = initial_norm * hessen[0]
    factor = jnp.linalg.cholesky(normal)
    size_of = len(columns)
    forward = []
    for row_at in range(size_of):
        running = target[row_at]
        for inner_at in range(row_at):
            running = running - factor[row_at, inner_at] * forward[inner_at]
        forward.append(running / factor[row_at, row_at])
    backward = [None] * size_of
    for row_at in reversed(range(size_of)):
        running = forward[row_at]
        for inner_at in range(row_at + 1, size_of):
            running = running - factor[inner_at, row_at] * backward[inner_at]
        backward[row_at] = running / factor[row_at, row_at]
    weights = jnp.stack(backward)
    leading = jnp.zeros((size_of + 1,), jnp.float32).at[0].set(initial_norm)
    misfit = leading - jnp.dot(hessen, weights, precision=lax.Precision.HIGHEST)
    return (backward, misfit)


def inside_along(index_now, count, cells):
    position = index_now * cells + jnp.arange(cells + 6, dtype=jnp.int32) - 3
    return (position >= 0) & (position < cells * count)


def shards(viscosity, force):
    cells_x, cells_y, cells_z = viscosity.shape
    eta_wide = extended(viscosity, (("gx", 0), ("gy", 1), (GZ, 2)), 4)
    wide_stencil = coefficients(eta_wide)
    stencil = tuple((member[3:-3, 3:-3, 3:-3] for member in wide_stencil))
    inside = (
        inside_along(lax.axis_index("gx"), lax.axis_size("gx"), cells_x)[:, None, None]
        & inside_along(lax.axis_index("gy"), lax.axis_size("gy"), cells_y)[None, :, None]
        & inside_along(lax.axis_index(GZ), lax.axis_size(GZ), cells_z)[None, None, :]
    ).astype(jnp.float32)
    wide_inverse = inside / (wide_stencil[6] + 1.0 - inside)

    def wide_block(update):
        return viscous(pad_cells(update), wide_stencil)

    rhs_full = jnp.concatenate([force, jnp.zeros((1,) + viscosity.shape, jnp.float32)], axis=0)
    initial_norm = jnp.sqrt(one_axis_at_a_time(jnp.sum(rhs_full * rhs_full), GX_GY_GZ))
    krylov = [rhs_full / initial_norm]
    search = []
    columns = []
    for column_at in range(ITERS):
        current = krylov[column_at]
        widened = extended(current[:3], (("gx", 1), ("gy", 2), (GZ, 3)), 3)
        smoothed = chebyshev(widened, wide_inverse, wide_block)[:, 3:-3, 3:-3, 3:-3]
        direction = jnp.concatenate([smoothed, (viscosity * current[3])[None]], axis=0)
        search.append(direction)
        bordered = with_halo(direction, (("gx", 1), ("gy", 2), (GZ, 3)), 1)
        candidate = stokes(bordered, stencil)
        local_products = jnp.stack([jnp.sum(candidate * vector) for vector in krylov])
        products, squared = (
            one_axis_at_a_time(local_products, GX_GY_GZ),
            one_axis_at_a_time(jnp.sum(candidate * candidate), GX_GY_GZ),
        )
        for row_at in range(column_at + 1):
            candidate = candidate - products[row_at] * krylov[row_at]
        length = jnp.sqrt(squared - jnp.sum(products * products))
        krylov.append(candidate / length)
        columns.append(
            jnp.concatenate(
                [products, length[None], jnp.zeros((ITERS - 1 - column_at,), jnp.float32)]
            )
        )
    weights, misfit = least_squares(columns, initial_norm)
    solution = weights[0] * search[0]
    column_at = 1
    solution = solution + weights[column_at] * search[column_at]
    residual = misfit[0] * krylov[0]
    for row_at in range(1, ITERS + 1):
        residual = residual + misfit[row_at] * krylov[row_at]
    return (solution, residual)


def solution(mesh):
    finer = Mesh(
        mesh.devices.reshape(mesh.shape["gx"], mesh.shape["gy"], 4, 2), ("gx", "gy", "gz_0", "gz_1")
    )
    return jax.shard_map(
        shards,
        mesh=finer,
        in_specs=(P("gx", "gy", GZ), P(None, "gx", "gy", GZ)),
        out_specs=(P(None, "gx", "gy", GZ), P(None, "gx", "gy", GZ)),
        check_vma=False,
    )
```

profile of v0, /device:TPU:1, one launch (start us, length us, event | category | flops | bytes accessed | tf_op | source)
XLA Modules:
  0.0 439.6 jit_solution(1423022594982378655)
XLA Ops:
  2.9 9.9 %psum.140 = f32[]{:T(128)} all-reduce(f32[]{:T(128)} %fusion.41), channel_id=1, replica_groups=mesh['gx'=4,'gy'=8,'gz_0'=4,'gz_1'=2] {'gx'}, use_global_device_ids=true, to_apply=%region_1.0 | all-reduce | flops 1 | bytes 8 | tf_op jit(solution)/shard_map/psum | solution.py:36
  13.6 16.9 %psum.141 = f32[]{:T(128)} all-reduce(f32[]{:T(128)} %psum.140), channel_id=1, replica_groups=mesh['gx'=4,'gy'=8,'gz_0'=4,'gz_1'=2] {'gy'}, use_global_device_ids=true, to_apply=%region_2.0 | all-reduce | flops 1 | bytes 8 | tf_op jit(solution)/shard_map/psum | solution.py:36
  31.7 9.4 %psum.142 = f32[]{:T(128)} all-reduce(f32[]{:T(128)} %psum.141), channel_id=1, replica_groups=mesh['gx'=4,'gy'=8,'gz_0'=4,'gz_1'=2] {'gz_0'}, use_global_device_ids=true, to_apply=%region_3.0 | all-reduce | flops 1 | bytes 8 | tf_op jit(solution)/shard_map/psum | solution.py:36
  45.1 11.8 %psum.143 = f32[]{:T(128)} all-reduce(f32[]{:T(128)} %psum.142), channel_id=1, replica_groups=mesh['gx'=4,'gy'=8,'gz_0'=4,'gz_1'=2] {'gz_1'}, use_global_device_ids=true, to_apply=%region_4.0 | all-reduce | flops 1 | bytes 8 | tf_op jit(solution)/shard_map/psum | solution.py:36
  128.6 5.0 %multiply_multiply_fusion.1 = f32[3,38,22,134]{3,1,2,0:T(8,128)} fusion(f32[38,22,134]{2,0,1:T(8,128)} %copy.317, f32[3,38,22,3]{3,1,2,0:T(8,128)} %copy.316, f32[3,38,3,128]{3,1,2,0:T(8,128)} %copy-done.59, f32[3,3,16,128]{3,1,2,0:T(4,128)} %copy-done.36, f32[3,32,16,128]{3,1,2,0:T(8,128)S(1)} %copy-done.14, f32[3,3,16,128]{3,1,2,0:T(4,128)} %copy-done.37, ...), kind=kLoop, calls=%fused_computation.95 | loop fusion | flops 2688576 | bytes 3136672 | tf_op jit(solution)/shard_map/div | solution.py:109
  133.6 13.4 %multiply_add_fusion.3 = (f32[3,38,22,134]{3,1,2,0:T(8,128)}, f32[3,38,22,134]{3,1,2,0:T(8,128)}) fusion(f32[38,22,134]{2,0,1:T(8,128)} %copy.325, f32[38,22,134]{2,0,1:T(8,128)} %copy.317, f32[3,38,22,3]{3,1,2,0:T(8,128)} %copy.316, f32[3,38,3,128]{3,1,2,0:T(8,128)} %copy-done.59, f32[3,3,16,128]{3,1,2,0:T(4,128)} %copy-done.36, ...), kind=kLoop, calls=%fused_computation.80 | loop fusion | flops 8065728 | bytes 9410016 | tf_op jit(solution)/shard_map/add | solution.py:116
  147.1 13.8 %multiply_add_fusion.2 = (f32[3,38,22,134]{3,1,2,0:T(8,128)}, f32[3,38,22,134]{3,1,2,0:T(8,128)}) fusion(f32[3,38,22,134]{3,1,2,0:T(8,128)} %get-tuple-element.56, f32[38,22,134]{2,0,1:T(8,128)} %copy.327, f32[3,38,22,134]{3,1,2,0:T(8,128)} %get-tuple-element.57, f32[38,22,134]{2,0,1:T(8,128)} %copy-done.10, f32[38,22,134]{2,0,1:T(8,128)} %copy.323, ...), kind=kLoop, calls=%fused_computation.66 | loop fusion | flops 5713224 | bytes 8961920 | tf_op jit(solution)/shard_map/add | solution.py:116
  160.9 11.0 %multiply_subtract_fusion.1 = (f32[3,38,22,134]{3,1,2,0:T(8,128)S(1)}, f32[3,38,22,134]{3,1,2,0:T(8,128)}, f32[3,38,22,134]{3,1,2,0:T(8,128)}) fusion(f32[3,38,22,134]{3,1,2,0:T(8,128)} %get-tuple-element.54, f32[38,22,134]{2,0,1:T(8,128)} %copy.326, f32[38,22,134]{2,0,1:T(8,128)S(1)} %copy-done, f32[38,22,134]{2,0,1:T(8,128)S(1)} %copy.321, ...), kind=kLoop, calls=%fused_computation.58 | loop fusion | flops 3360720 | bytes 8065728 | tf_op jit(solution)/shard_map/sub | solution.py:76
  171.9 6.1 %fusion.75 = f32[3,32,16,128]{3,1,2,0:T(8,128)S(1)} fusion(f32[3,38,22,134]{3,1,2,0:T(8,128)} %get-tuple-element.56, f32[3,38,22,134]{3,1,2,0:T(8,128)} %multiply_multiply_fusion.1, f32[3,38,22,134]{3,1,2,0:T(8,128)} %get-tuple-element.55, f32[3,38,22,134]{3,1,2,0:T(8,128)} %get-tuple-element.63, f32[3,38,22,134]{3,1,2,0:T(8,128)} %get-tuple-element.62, ...), kind=kLoop, calls=%fused_computation.191 | loop fusion | flops 1966080 | bytes 6815744 | tf_op jit(solution)/shard_map/add | solution.py:118
  216.2 6.6 %all-reduce.21 = (f32[]{:T(128)}, f32[1]{0:T(128)}) all-reduce(f32[]{:T(128)} %get-tuple-element.24, f32[1]{0:T(128)} %bitcast.12), channel_id=1, replica_groups=mesh['gx'=4,'gy'=8,'gz_0'=4,'gz_1'=2] {'gx'}, use_global_device_ids=true, to_apply=%region_11.12 | all-reduce | flops 2 | bytes 16 | tf_op jit(solution)/shard_map/psum | solution.py:36
  222.8 14.3 %all-reduce.17 = (f32[]{:T(128)}, f32[1]{0:T(128)}) all-reduce(f32[]{:T(128)} %get-tuple-element.35, f32[1]{0:T(128)} %get-tuple-element.36), channel_id=1, replica_groups=mesh['gx'=4,'gy'=8,'gz_0'=4,'gz_1'=2] {'gy'}, use_global_device_ids=true, to_apply=%region_12.13 | all-reduce | flops 2 | bytes 16 | tf_op jit(solution)/shard_map/psum | solution.py:36
  237.1 7.0 %all-reduce.19 = (f32[]{:T(128)}, f32[1]{0:T(128)}) all-reduce(f32[]{:T(128)} %get-tuple-element.27, f32[1]{0:T(128)} %get-tuple-element.28), channel_id=1, replica_groups=mesh['gx'=4,'gy'=8,'gz_0'=4,'gz_1'=2] {'gz_0'}, use_global_device_ids=true, to_apply=%region_13.14 | all-reduce | flops 2 | bytes 16 | tf_op jit(solution)/shard_map/psum | solution.py:36
  244.1 11.7 %all-reduce.23 = (f32[]{:T(128)}, f32[1]{0:T(128)}) all-reduce(f32[]{:T(128)} %get-tuple-element.31, f32[1]{0:T(128)} %get-tuple-element.32), channel_id=1, replica_groups=mesh['gx'=4,'gy'=8,'gz_0'=4,'gz_1'=2] {'gz_1'}, use_global_device_ids=true, to_apply=%region_14.15 | all-reduce | flops 2 | bytes 16 | tf_op jit(solution)/shard_map/psum | solution.py:36
  271.5 4.4 collective-permute-done.21
  297.0 5.3 %multiply_multiply_fusion = f32[3,38,22,134]{3,1,2,0:T(8,128)} fusion(f32[38,22,134]{2,0,1:T(8,128)} %copy.317, f32[3,38,22,3]{3,1,2,0:T(8,128)} %copy.353, f32[3,38,3,128]{3,1,2,0:T(8,128)} %copy-done.61, f32[3,3,16,128]{3,1,2,0:T(4,128)} %copy-done.38, f32[3,32,16,128]{3,1,2,0:T(8,128)} %copy-done.15, f32[3,3,16,128]{3,1,2,0:T(4,128)} %copy-done.39, ...), kind=kLoop, calls=%fused_computation.94 | loop fusion | flops 2688576 | bytes 3136672 | tf_op jit(solution)/shard_map/div | solution.py:109
  302.2 13.4 %multiply_add_fusion.1 = (f32[3,38,22,134]{3,1,2,0:T(8,128)}, f32[3,38,22,134]{3,1,2,0:T(8,128)}) fusion(f32[38,22,134]{2,0,1:T(8,128)} %copy.325, f32[38,22,134]{2,0,1:T(8,128)} %copy.317, f32[3,38,22,3]{3,1,2,0:T(8,128)} %copy.353, f32[3,38,3,128]{3,1,2,0:T(8,128)} %copy-done.61, f32[3,3,16,128]{3,1,2,0:T(4,128)} %copy-done.38, ...), kind=kLoop, calls=%fused_computation.43 | loop fusion | flops 8065728 | bytes 9410016 | tf_op jit(solution)/shard_map/add | solution.py:116
  315.7 13.8 %multiply_add_fusion = (f32[3,38,22,134]{3,1,2,0:T(8,128)}, f32[3,38,22,134]{3,1,2,0:T(8,128)}) fusion(f32[3,38,22,134]{3,1,2,0:T(8,128)} %get-tuple-element.43, f32[38,22,134]{2,0,1:T(8,128)} %copy.327, f32[3,38,22,134]{3,1,2,0:T(8,128)} %get-tuple-element.44, f32[38,22,134]{2,0,1:T(8,128)} %copy-done.10, f32[38,22,134]{2,0,1:T(8,128)} %copy.323, ...), kind=kLoop, calls=%fused_computation.29 | loop fusion | flops 5713224 | bytes 8961920 | tf_op jit(solution)/shard_map/add | solution.py:116
  329.5 11.2 %multiply_subtract_fusion = (f32[3,38,22,134]{3,1,2,0:T(8,128)S(1)}, f32[3,38,22,134]{3,1,2,0:T(8,128)}, f32[3,38,22,134]{3,1,2,0:T(8,128)}) fusion(f32[3,38,22,134]{3,1,2,0:T(8,128)} %get-tuple-element.41, f32[38,22,134]{2,0,1:T(8,128)} %copy.326, f32[38,22,134]{2,0,1:T(8,128)S(1)} %copy-done.1, f32[38,22,134]{2,0,1:T(8,128)S(1)} %copy.321, ...), kind=kLoop, calls=%fused_computation.21 | loop fusion | flops 3360720 | bytes 8065728 | tf_op jit(solution)/shard_map/sub | solution.py:76
  340.6 6.1 %fusion.63 = f32[3,32,16,128]{3,1,2,0:T(8,128)S(1)} fusion(f32[3,38,22,134]{3,1,2,0:T(8,128)} %get-tuple-element.43, f32[3,38,22,134]{3,1,2,0:T(8,128)} %multiply_multiply_fusion, f32[3,38,22,134]{3,1,2,0:T(8,128)} %get-tuple-element.42, f32[3,38,22,134]{3,1,2,0:T(8,128)} %get-tuple-element.60, f32[3,38,22,134]{3,1,2,0:T(8,128)} %get-tuple-element.59, ...), kind=kLoop, calls=%fused_computation.169 | loop fusion | flops 1966080 | bytes 6815744 | tf_op jit(solution)/shard_map/add | solution.py:118
  355.9 4.6 %collective-permute-start.29 = (f32[4,32,16,1]{1,2,3,0:T(8,128)S(1)}, f32[4,32,16,1]{1,2,3,0:T(8,128)S(1)}, u32[]{:S(2)}, u32[]{:S(2)}) collective-permute-start(f32[4,32,16,1]{1,2,3,0:T(8,128)S(1)} %copy.363), channel_id=1, source_target_pairs={{0,1},{1,2},{2,3},{3,4},{4,5},{5,6},{6,7},{8,9},{9,10},{10,11},{11... | collective-permute-start | bytes 24584 | tf_op jit(solution)/shard_map/ppermute | solution.py:48
  377.9 8.3 %all-reduce.20 = (f32[]{:T(128)}, f32[2]{0:T(128)S(1)}) all-reduce(f32[]{:T(128)} %get-tuple-element.22, f32[2]{0:T(128)S(1)} %pad_maximum_fusion.45), channel_id=1, replica_groups=mesh['gx'=4,'gy'=8,'gz_0'=4,'gz_1'=2] {'gx'}, use_global_device_ids=true, to_apply=%region_22.23 | all-reduce | flops 3 | bytes 24 | tf_op jit(solution)/shard_map/psum | solution.py:36
  386.2 15.9 %all-reduce.16 = (f32[]{:T(128)}, f32[2]{0:T(128)S(1)}) all-reduce(f32[]{:T(128)} %get-tuple-element.33, f32[2]{0:T(128)S(1)} %get-tuple-element.34), channel_id=1, replica_groups=mesh['gx'=4,'gy'=8,'gz_0'=4,'gz_1'=2] {'gy'}, use_global_device_ids=true, to_apply=%region_23.24 | all-reduce | flops 3 | bytes 24 | tf_op jit(solution)/shard_map/psum | solution.py:36
  402.1 6.9 %all-reduce.18 = (f32[]{:T(128)}, f32[2]{0:T(128)S(1)}) all-reduce(f32[]{:T(128)} %get-tuple-element.25, f32[2]{0:T(128)S(1)} %get-tuple-element.26), channel_id=1, replica_groups=mesh['gx'=4,'gy'=8,'gz_0'=4,'gz_1'=2] {'gz_0'}, use_global_device_ids=true, to_apply=%region_24.25 | all-reduce | flops 3 | bytes 24 | tf_op jit(solution)/shard_map/psum | solution.py:36
  409.0 11.9 %all-reduce.22 = (f32[]{:T(128)}, f32[2]{0:T(128)S(1)}) all-reduce(f32[]{:T(128)} %get-tuple-element.29, f32[2]{0:T(128)S(1)} %get-tuple-element.30), channel_id=1, replica_groups=mesh['gx'=4,'gy'=8,'gz_0'=4,'gz_1'=2] {'gz_1'}, use_global_device_ids=true, to_apply=%region_25.26 | all-reduce | flops 3 | bytes 24 | tf_op jit(solution)/shard_map/psum | solution.py:36
  (315 shorter events, 189.8 us)
Async XLA Ops:
  30.4 33.7 %collective-permute-start.1 = (f32[4,16,128]{2,1,0:T(8,128)S(1)}, f32[4,16,128]{2,1,0:T(8,128)S(1)}, u32[]{:S(2)}, u32[]{:S(2)}) collective-permute-start(f32[4,16,128]{2,1,0:T(8,128)S(1)} %get-tuple-element.108), channel_id=1, source_target_pairs={{64,0},{128,64},{192,128},{65,1},{129,65},{193,129},{66,2},{130,66... | collective-permute-start | bytes 98312 | tf_op jit(solution)/shard_map/ppermute | solution.py:27
  41.1 23.0 %collective-permute-start = (f32[4,16,128]{2,1,0:T(8,128)S(1)}, f32[4,16,128]{2,1,0:T(8,128)S(1)}, u32[]{:S(2)}, u32[]{:S(2)}) collective-permute-start(f32[4,16,128]{2,1,0:T(8,128)S(1)} %get-tuple-element.109), channel_id=1, source_target_pairs={{0,64},{64,128},{128,192},{1,65},{65,129},{129,193},{2,66},{66,130... | collective-permute-start | bytes 98312 | tf_op jit(solution)/shard_map/ppermute | solution.py:25
  57.8 9.2 %collective-permute-start.7 = (f32[3,3,16,128]{3,2,1,0:T(8,128)S(1)}, f32[3,3,16,128]{3,2,1,0:T(8,128)S(1)}, u32[]{:S(2)}, u32[]{:S(2)}) collective-permute-start(f32[3,3,16,128]{3,2,1,0:T(8,128)S(1)} %copy.310), channel_id=1, source_target_pairs={{64,0},{128,64},{192,128},{65,1},{129,65},{193,129},{66,2},{130,66... | collective-permute-start | bytes 221192 | tf_op jit(solution)/shard_map/ppermute | solution.py:27
  59.1 7.9 %collective-permute-start.6 = (f32[3,3,16,128]{3,2,1,0:T(8,128)S(1)}, f32[3,3,16,128]{3,2,1,0:T(8,128)S(1)}, u32[]{:S(2)}, u32[]{:S(2)}) collective-permute-start(f32[3,3,16,128]{3,2,1,0:T(8,128)S(1)} %copy.309), channel_id=1, source_target_pairs={{0,64},{64,128},{128,192},{1,65},{65,129},{129,193},{2,66},{66,130... | collective-permute-start | bytes 221192 | tf_op jit(solution)/shard_map/ppermute | solution.py:25
  71.1 9.6 %collective-permute-start.4 = (f32[40,24,4]{2,1,0:T(8,128)S(1)}, f32[40,24,4]{2,1,0:T(8,128)S(1)}, u32[]{:S(2)}, u32[]{:S(2)}) collective-permute-start(f32[40,24,4]{2,1,0:T(8,128)S(1)} %get-tuple-element.104), channel_id=1, source_target_pairs={{0,1},{1,2},{2,3},{3,4},{4,5},{5,6},{6,7},{8,9},{9,10},{10,11},{11... | collective-permute-start | bytes 46088 | tf_op jit(solution)/shard_map/ppermute | solution.py:25
  74.4 10.4 %collective-permute-start.5 = (f32[40,24,4]{2,1,0:T(8,128)S(1)}, f32[40,24,4]{2,1,0:T(8,128)S(1)}, u32[]{:S(2)}, u32[]{:S(2)}) collective-permute-start(f32[40,24,4]{2,1,0:T(8,128)S(1)} %get-tuple-element.105), channel_id=1, source_target_pairs={{1,0},{2,1},{3,2},{4,3},{5,4},{6,5},{7,6},{9,8},{10,9},{11,10},{12... | collective-permute-start | bytes 46088 | tf_op jit(solution)/shard_map/ppermute | solution.py:27
  76.7 13.7 %collective-permute-start.8 = (f32[3,38,3,128]{3,1,2,0:T(8,128)S(1)}, f32[3,38,3,128]{3,1,2,0:T(8,128)S(1)}, u32[]{:S(2)}, u32[]{:S(2)}) collective-permute-start(f32[3,38,3,128]{3,1,2,0:T(8,128)S(1)} %get-tuple-element.94), channel_id=1, source_target_pairs={{0,8},{8,16},{16,24},{24,32},{32,40},{40,48},{48,56},{1,9},{9,17},... | collective-permute-start | bytes 525320 | tf_op jit(solution)/shard_map/ppermute | solution.py:25
  79.3 11.0 %collective-permute-start.9 = (f32[3,38,3,128]{3,1,2,0:T(8,128)S(1)}, f32[3,38,3,128]{3,1,2,0:T(8,128)S(1)}, u32[]{:S(2)}, u32[]{:S(2)}) collective-permute-start(f32[3,38,3,128]{3,1,2,0:T(8,128)S(1)} %get-tuple-element.95), channel_id=1, source_target_pairs={{8,0},{16,8},{24,16},{32,24},{40,32},{48,40},{56,48},{9,1},{17,9},... | collective-permute-start | bytes 525320 | tf_op jit(solution)/shard_map/ppermute | solution.py:27
  95.9 30.1 %collective-permute-start.11 = (f32[3,38,22,3]{1,2,3,0:T(8,128)}, f32[3,38,22,3]{1,2,3,0:T(8,128)}, u32[]{:S(2)}, u32[]{:S(2)}) collective-permute-start(f32[3,38,22,3]{1,2,3,0:T(8,128)} %copy.314), channel_id=1, source_target_pairs={{1,0},{2,1},{3,2},{4,3},{5,4},{6,5},{7,6},{9,8},{10,9},{11,10},{12... | collective-permute-start | bytes 90296 | tf_op jit(solution)/shard_map/ppermute | solution.py:27
  98.0 25.5 %collective-permute-start.10 = (f32[3,38,22,3]{1,2,3,0:T(8,128)}, f32[3,38,22,3]{1,2,3,0:T(8,128)}, u32[]{:S(2)}, u32[]{:S(2)}) collective-permute-start(f32[3,38,22,3]{1,2,3,0:T(8,128)} %copy.313), channel_id=1, source_target_pairs={{0,1},{1,2},{2,3},{3,4},{4,5},{5,6},{6,7},{8,9},{9,10},{10,11},{11... | collective-permute-start | bytes 90296 | tf_op jit(solution)/shard_map/ppermute | solution.py:25
  180.3 29.5 %collective-permute-start.12 = (f32[4,1,16,128]{3,2,1,0:T(8,128)}, f32[4,1,16,128]{3,2,1,0:T(8,128)S(1)}, u32[]{:S(2)}, u32[]{:S(2)}) collective-permute-start(f32[4,1,16,128]{3,2,1,0:T(8,128)} %bitcast.2), channel_id=1, source_target_pairs={{64,0},{128,64},{192,128},{65,1},{129,65},{193,129},{66,2},{130,66... | collective-permute-start | bytes 98312 | tf_op jit(solution)/shard_map/ppermute | solution.py:49
  181.6 28.3 %collective-permute-start.13 = (f32[4,1,16,128]{3,2,1,0:T(8,128)}, f32[4,1,16,128]{3,2,1,0:T(8,128)S(1)}, u32[]{:S(2)}, u32[]{:S(2)}) collective-permute-start(f32[4,1,16,128]{3,2,1,0:T(8,128)} %bitcast.4), channel_id=1, source_target_pairs={{0,64},{64,128},{128,192},{1,65},{65,129},{129,193},{2,66},{66,130... | collective-permute-start | bytes 98312 | tf_op jit(solution)/shard_map/ppermute | solution.py:48
  190.2 16.0 %collective-permute-start.17 = (f32[4,32,16,1]{1,2,3,0:T(8,128)}, f32[4,32,16,1]{1,2,3,0:T(8,128)}, u32[]{:S(2)}, u32[]{:S(2)}) collective-permute-start(f32[4,32,16,1]{1,2,3,0:T(8,128)} %copy.344), channel_id=1, source_target_pairs={{0,1},{1,2},{2,3},{3,4},{4,5},{5,6},{6,7},{8,9},{9,10},{10,11},{11... | collective-permute-start | bytes 24584 | tf_op jit(solution)/shard_map/ppermute | solution.py:48
  192.6 7.1 %collective-permute-start.16 = (f32[4,32,16,1]{1,2,3,0:T(8,128)}, f32[4,32,16,1]{1,2,3,0:T(8,128)}, u32[]{:S(2)}, u32[]{:S(2)}) collective-permute-start(f32[4,32,16,1]{1,2,3,0:T(8,128)} %copy.341), channel_id=1, source_target_pairs={{1,0},{2,1},{3,2},{4,3},{5,4},{6,5},{7,6},{9,8},{10,9},{11,10},{12... | collective-permute-start | bytes 24584 | tf_op jit(solution)/shard_map/ppermute | solution.py:49
  196.5 13.7 %collective-permute-start.15 = (f32[4,32,1,128]{3,1,2,0:T(8,128)}, f32[4,32,1,128]{3,1,2,0:T(8,128)}, u32[]{:S(2)}, u32[]{:S(2)}) collective-permute-start(f32[4,32,1,128]{3,1,2,0:T(8,128)} %get-tuple-element.88), channel_id=1, source_target_pairs={{0,8},{8,16},{16,24},{24,32},{32,40},{40,48},{48,56},{1,9},{9,17},... | collective-permute-start | bytes 196616 | tf_op jit(solution)/shard_map/ppermute | solution.py:48
  199.7 11.3 %collective-permute-start.14 = (f32[4,32,1,128]{3,1,2,0:T(8,128)}, f32[4,32,1,128]{3,1,2,0:T(8,128)}, u32[]{:S(2)}, u32[]{:S(2)}) collective-permute-start(f32[4,32,1,128]{3,1,2,0:T(8,128)} %get-tuple-element.89), channel_id=1, source_target_pairs={{8,0},{16,8},{24,16},{32,24},{40,32},{48,40},{56,48},{9,1},{17,9},... | collective-permute-start | bytes 196616 | tf_op jit(solution)/shard_map/ppermute | solution.py:49
  259.9 6.0 %collective-permute-start.19 = (f32[3,3,16,128]{3,2,1,0:T(8,128)S(1)}, f32[3,3,16,128]{3,2,1,0:T(8,128)S(1)}, u32[]{:S(2)}, u32[]{:S(2)}) collective-permute-start(f32[3,3,16,128]{3,2,1,0:T(8,128)S(1)} %copy.347), channel_id=1, source_target_pairs={{64,0},{128,64},{192,128},{65,1},{129,65},{193,129},{66,2},{130,66... | collective-permute-start | bytes 221192 | tf_op jit(solution)/shard_map/ppermute | solution.py:27
  268.8 7.1 %collective-permute-start.21 = (f32[3,38,3,128]{3,1,2,0:T(8,128)S(1)}, f32[3,38,3,128]{3,1,2,0:T(8,128)S(1)}, u32[]{:S(2)}, u32[]{:S(2)}) collective-permute-start(f32[3,38,3,128]{3,1,2,0:T(8,128)S(1)} %get-tuple-element.93), channel_id=1, source_target_pairs={{8,0},{16,8},{24,16},{32,24},{40,32},{48,40},{56,48},{9,1},{17,9},... | collective-permute-start | bytes 525320 | tf_op jit(solution)/shard_map/ppermute | solution.py:27
  283.8 10.6 %collective-permute-start.23 = (f32[3,38,22,3]{1,2,3,0:T(8,128)}, f32[3,38,22,3]{1,2,3,0:T(8,128)}, u32[]{:S(2)}, u32[]{:S(2)}) collective-permute-start(f32[3,38,22,3]{1,2,3,0:T(8,128)} %copy.351), channel_id=1, source_target_pairs={{1,0},{2,1},{3,2},{4,3},{5,4},{6,5},{7,6},{9,8},{10,9},{11,10},{12... | collective-permute-start | bytes 90296 | tf_op jit(solution)/shard_map/ppermute | solution.py:27
  348.2 21.9 %collective-permute-start.24 = (f32[4,1,16,128]{3,2,1,0:T(8,128)S(1)}, f32[4,1,16,128]{3,2,1,0:T(8,128)S(1)}, u32[]{:S(2)}, u32[]{:S(2)}) collective-permute-start(f32[4,1,16,128]{3,2,1,0:T(8,128)S(1)} %bitcast.103), channel_id=1, source_target_pairs={{64,0},{128,64},{192,128},{65,1},{129,65},{193,129},{66,2},{130,66... | collective-permute-start | bytes 98312 | tf_op jit(solution)/shard_map/ppermute | solution.py:49
  349.5 20.6 %collective-permute-start.25 = (f32[4,1,16,128]{3,2,1,0:T(8,128)S(1)}, f32[4,1,16,128]{3,2,1,0:T(8,128)S(1)}, u32[]{:S(2)}, u32[]{:S(2)}) collective-permute-start(f32[4,1,16,128]{3,2,1,0:T(8,128)S(1)} %bitcast.102), channel_id=1, source_target_pairs={{0,64},{64,128},{128,192},{1,65},{65,129},{129,193},{2,66},{66,130... | collective-permute-start | bytes 98312 | tf_op jit(solution)/shard_map/ppermute | solution.py:48
  355.9 13.5 %collective-permute-start.29 = (f32[4,32,16,1]{1,2,3,0:T(8,128)S(1)}, f32[4,32,16,1]{1,2,3,0:T(8,128)S(1)}, u32[]{:S(2)}, u32[]{:S(2)}) collective-permute-start(f32[4,32,16,1]{1,2,3,0:T(8,128)S(1)} %copy.363), channel_id=1, source_target_pairs={{0,1},{1,2},{2,3},{3,4},{4,5},{5,6},{6,7},{8,9},{9,10},{10,11},{11... | collective-permute-start | bytes 24584 | tf_op jit(solution)/shard_map/ppermute | solution.py:48
  362.5 7.8 %collective-permute-start.27 = (f32[4,32,1,128]{3,1,2,0:T(8,128)S(1)}, f32[4,32,1,128]{3,1,2,0:T(8,128)S(1)}, u32[]{:S(2)}, u32[]{:S(2)}) collective-permute-start(f32[4,32,1,128]{3,1,2,0:T(8,128)S(1)} %get-tuple-element.78), channel_id=1, source_target_pairs={{0,8},{8,16},{16,24},{24,32},{32,40},{40,48},{48,56},{1,9},{9,17},... | collective-permute-start | bytes 196616 | tf_op jit(solution)/shard_map/ppermute | solution.py:48
  366.1 5.7 %collective-permute-start.26 = (f32[4,32,1,128]{3,1,2,0:T(8,128)S(1)}, f32[4,32,1,128]{3,1,2,0:T(8,128)S(1)}, u32[]{:S(2)}, u32[]{:S(2)}) collective-permute-start(f32[4,32,1,128]{3,1,2,0:T(8,128)S(1)} %get-tuple-element.79), channel_id=1, source_target_pairs={{8,0},{16,8},{24,16},{32,24},{40,32},{48,40},{56,48},{9,1},{17,9},... | collective-permute-start | bytes 196616 | tf_op jit(solution)/shard_map/ppermute | solution.py:49
  (68 other events, 547.5 us)
where the time goes:
time: 447 us; the launch traced here: 440 us
  blocking collectives  131 us (29%)
  other arithmetic  130 us (29%)
  starting transfers between devices  75.9 us (17%)
  local copies, waits for them, and re-layouts  74.2 us (17%)
  waiting for transfers between devices  17.1 us (4%)
  between operations  11.2 us (3%)
    psum x12, blocking collectives, one_axis_at_a_time(): shard = lax.psum(shard, axis)  131 us
    add x4, other arithmetic, chebyshev(): ratio_next * ratio_now * update  54.4 us
    ppermute x9, starting transfers between devices, extended(): lax.ppermute(tail, axis, [(i, (i + 1) % count) for i in range(ends)])  27.3 us
    ppermute x6, starting transfers between devices, with_halo(): lax.ppermute(last, axis, up)  22.3 us
    sub x2, other arithmetic, viscous(): result - y_plus * padded[:, 1:-1, 2:, 1:-1]  22.1 us
    ppermute x9, starting transfers between devices, extended(): lax.ppermute(head, axis, [((i + 1) % count, i) for i in range(ends)])  16.1 us
    ppermute x9, waiting for transfers between devices, extended(): lax.ppermute(head, axis, [((i + 1) % count, i) for i in range(ends)])  12.6 us
    add x2, other arithmetic, chebyshev(): result = result + update  12.2 us
  transfers between devices with their start and end apart: 30, of which 8 were waited for; matrix products, arithmetic and copies ran while one was open for 12% of the time, Pallas kernels for 0%

commit v1 on v0

v1 whole, which is shorter than its diff:
```python
import functools

import jax
import jax.numpy as jnp
from jax import lax
from jax.experimental import pallas as pl
from jax.experimental.pallas import tpu as pltpu
from jax.sharding import PartitionSpec as P

CHEB = 4
LOW_EDGE = 0.25
HIGH_EDGE = 2.0
MIDDLE = 0.5 * (HIGH_EDGE + LOW_EDGE)
HALF = 0.5 * (HIGH_EDGE - LOW_EDGE)
AXES = ("gx", "gy", "gz")

BX, BY, BZ, H = 32, 16, 128, 8
EX, EY, EZ = BX + 2 * H, BY + 2 * H, BZ + 2 * H
CHUNKS = 4
SLABS = EX // CHUNKS
LANES = CHUNKS * EY
ROWS = EZ + 16
YTILES = 4 * EX + BX // 8
ZTILES = 4 * SLABS + 2
OWN = slice(16, 16 + BZ)
PIECES = [(8, 8)] + [(16 + 16 * i, 16) for i in range(8)] + [(144, 8)]
OWN_PIECES = PIECES[1:-1]


def chebyshev_factors():
    scaled = MIDDLE / HALF
    now = 1.0 / scaled
    pairs = []
    for _ in range(CHEB - 1):
        following = 1.0 / (2.0 * scaled - now)
        pairs.append((following * now, 2.0 * following / HALF))
        now = following
    return pairs


def pack_y(force, visc, low_x, high_x, tail, head):
    for out, first in ((tail, BY - 8), (head, 0)):
        rows = slice(first, first + 8)
        for c in range(3):
            base = c * EX
            out[base : base + 8] = low_x[c * 8 : c * 8 + 8, rows, :]
            out[base + 8 : base + 8 + BX] = force[c, :, rows, :]
            out[base + 8 + BX : base + EX] = high_x[c * 8 : c * 8 + 8, rows, :]
        base = 3 * EX
        out[base : base + 8] = low_x[25:33, rows, :]
        out[base + 8 : base + 8 + BX] = visc[:, rows, :]
        out[base + 8 + BX : base + EX] = high_x[24:32, rows, :]
        ninth = first - 1 if first else 8
        for x in range(BX):
            out[4 * EX + x // 8, x % 8, :] = visc[x, ninth, :]


def to_lanes(force, visc, low_x, high_x, low_y, high_y, f_out, v_out, ry_out, ex_out, tail, head):
    def rows_of(c, at):
        x = at - H
        if x < 0:
            middle = low_x[c * 8 + at] if c < 3 else low_x[25 + at]
        elif x >= BX:
            middle = high_x[c * 8 + x - BX] if c < 3 else high_x[24 + x - BX]
        else:
            middle = force[c, x] if c < 3 else visc[x]
        return [low_y[c * EX + at], middle, high_y[c * EX + at]]

    for c in range(4):
        for g in range(SLABS):
            parts = []
            for k in range(CHUNKS):
                parts += rows_of(c, k * SLABS + g)
            block = jnp.concatenate(parts, axis=0).T
            if c < 3:
                f_out[c, g] = block
            else:
                v_out[g] = block
                tail[4 * SLABS + g // 8, g % 8 : g % 8 + 1, :] = block[BZ - 9 : BZ - 8]
                head[4 * SLABS + g // 8, g % 8 : g % 8 + 1, :] = block[8:9]
            tail[c * SLABS + g] = block[BZ - 8 :]
            head[c * SLABS + g] = block[:8]
    for out in (tail, head):
        out[ZTILES - 1, SLABS - 8 :, :] = jnp.zeros((16 - SLABS, LANES), jnp.float32)
    nothing = jnp.zeros((EY - 2, BZ), jnp.float32)
    for g in range(SLABS):
        parts = []
        for k in range(CHUNKS):
            x = k * SLABS + g - H
            if 0 <= x < BX:
                at = 4 * EX + x // 8
                lower, upper = low_y[at, x % 8 : x % 8 + 1, :], high_y[at, x % 8 : x % 8 + 1, :]
            else:
                lower = upper = jnp.zeros((1, BZ), jnp.float32)
            parts += [lower, nothing, upper]
        ry_out[g] = jnp.concatenate(parts, axis=0).T
    side = jnp.zeros((8, BZ), jnp.float32)
    between = jnp.zeros((2 * EY, BZ), jnp.float32)
    ex_out[...] = jnp.concatenate(
        [side, low_x[24], side, between, side, high_x[32], side], axis=0
    ).T


def lane_index(rows):
    return lax.broadcasted_iota(jnp.int32, (rows, LANES), 1)


def solve_local(
    f, v, ry, ex, low_z, high_z,
    s0_out, u1_out, s1_out, u2_out, sums,
    visc, coef, inv, diag, d0, d1, d2, s, r, p,
):
    def place(g, _):
        visc[g + 1, 0:8] = jnp.zeros((8, LANES), jnp.float32)
        visc[g + 1, 152:160] = jnp.zeros((8, LANES), jnp.float32)
        visc[g + 1, 8:16] = low_z[3 * SLABS + g]
        visc[g + 1, OWN] = v[g]
        visc[g + 1, 144:152] = high_z[3 * SLABS + g]
        return 0

    lax.fori_loop(0, SLABS, place, 0)
    for g in range(SLABS):
        visc[g + 1, 7:8] = low_z[4 * SLABS + g // 8, g % 8 : g % 8 + 1, :]
        visc[g + 1, 152:153] = high_z[4 * SLABS + g // 8, g % 8 : g % 8 + 1, :]
    for first, count in PIECES:
        rows = slice(first, first + count)
        before = pltpu.roll(visc[SLABS, rows], EY, 1)
        after = pltpu.roll(visc[1, rows], LANES - EY, 1)
        if 16 <= first < 144:
            lane = lane_index(count)
            extra = ex[first - 16 : first - 16 + count]
            before = jnp.where(lane < EY, extra, before)
            after = jnp.where(lane >= LANES - EY, extra, after)
        visc[0, rows] = before
        visc[SLABS + 1, rows] = after

    def border(ref, which):
        zero = jnp.zeros((8, LANES), jnp.float32)
        for c in which:
            for g in range(SLABS):
                at = (c, g + 1) if c is not None else (g + 1,)
                ref[(*at, slice(0, 8))] = zero
                ref[(*at, slice(152, 160))] = zero

    for ref in (d0, d1, d2, s):
        border(ref, range(3))
    border(p, [None])

    def ghosts(ref, which):
        for c in which:
            for first, count in PIECES:
                rows = slice(first, first + count)
                pre = (c,) if c is not None else ()
                ref[(*pre, 0, rows)] = pltpu.roll(ref[(*pre, SLABS, rows)], EY, 1)
                ref[(*pre, SLABS + 1, rows)] = pltpu.roll(ref[(*pre, 1, rows)], LANES - EY, 1)

    def setup(g, _):
        at = g + 1
        for first, count in PIECES:
            rows = slice(first, first + count)
            here = slice(first - 8, first - 8 + count)
            lane = lane_index(count)
            y_at = lane & (EY - 1)
            mine = visc[at, rows]
            below, above = pltpu.roll(mine, 1, 1), pltpu.roll(mine, LANES - 1, 1)
            if 16 <= first < 144:
                extra = ry[g, first - 16 : first - 16 + count]
                below = jnp.where(y_at == 0, extra, below)
                above = jnp.where(y_at == EY - 1, extra, above)
            x_plus = 0.5 * (mine + visc[at + 1, rows])
            x_minus = 0.5 * (mine + visc[at - 1, rows])
            y_plus = 0.5 * (mine + above)
            y_minus = 0.5 * (mine + below)
            z_plus = 0.5 * (mine + visc[at, first + 1 : first + 1 + count])
            z_minus = 0.5 * (mine + visc[at, first - 1 : first - 1 + count])
            total = x_plus + x_minus + y_plus + y_minus + z_plus + z_minus
            inside = mine > 0.0
            inverse = jnp.where(inside, 1.0 / jnp.where(inside, total, 1.0), 0.0)
            inv[g, here] = inverse
            diag[g, here] = total
            for i, face in enumerate((x_minus, x_plus, y_minus, y_plus, z_minus, z_plus)):
                coef[i, g, here] = face * inverse
            for c in range(3):
                if first == 8:
                    value = low_z[c * SLABS + g]
                elif first == 144:
                    value = high_z[c * SLABS + g]
                else:
                    value = f[c, g, first - 16 : first - 16 + count]
                d0[c, at, rows] = value * inverse * (1.0 / MIDDLE)
        return 0

    lax.fori_loop(0, SLABS, setup, 0)
    ghosts(d0, range(3))

    def neighbours(ref, c, g, first, count):
        at = g + 1
        rows = slice(first, first + count)
        here = slice(first - 8, first - 8 + count)
        mine = ref[c, at, rows]
        below, above = pltpu.roll(mine, 1, 1), pltpu.roll(mine, LANES - 1, 1)
        x_minus, x_plus = ref[c, at - 1, rows], ref[c, at + 1, rows]
        z_minus = ref[c, at, first - 1 : first - 1 + count]
        z_plus = ref[c, at, first + 1 : first + 1 + count]
        total = coef[0, g, here] * x_minus + coef[1, g, here] * x_plus
        total = total + (coef[2, g, here] * below + coef[3, g, here] * above)
        total = total + (coef[4, g, here] * z_minus + coef[5, g, here] * z_plus)
        return mine, total, (x_minus, x_plus, below, above, z_minus, z_plus)

    def smooth():
        factors = chebyshev_factors()
        old = (d0, d1, d2)
        for step in range(CHEB - 1):
            scale_d, scale_r = factors[step]
            source = old[step]
            last = step == CHEB - 2

            def body(g, _):
                for first, count in PIECES:
                    rows = slice(first, first + count)
                    here = slice(first - 8, first - 8 + count)
                    for c in range(3):
                        mine, total, _ = neighbours(source, c, g, first, count)
                        if step == 0:
                            left = (MIDDLE - 1.0) * mine + total
                        else:
                            left = r[c, g, here] - mine + total
                        new = scale_d * mine + scale_r * left
                        if last:
                            s[c, g + 1, rows] = d0[c, g + 1, rows] + d1[c, g + 1, rows] + mine + new
                        else:
                            r[c, g, here] = left
                            old[step + 1][c, g + 1, rows] = new
                return 0

            lax.fori_loop(0, SLABS, body, 0)
            ghosts(s if last else old[step + 1], range(3))

    smooth()

    def apply_first(g, _):
        at = g + 1
        for first, count in PIECES:
            rows = slice(first, first + count)
            here = slice(first - 8, first - 8 + count)
            own = slice(first - 16, first - 16 + count)
            is_own = 16 <= first < 144
            flow = None
            for c in range(3):
                mine, total, sides = neighbours(s, c, g, first, count)
                value = diag[g, here] * (mine - total)
                slope = sides[2 * c + 1] - sides[2 * c]
                flow = slope if flow is None else flow + slope
                d0[c, at, rows] = value * inv[g, here] * (1.0 / MIDDLE)
                if is_own:
                    u1_out[c, g, own] = value
                    s0_out[c, g, own] = mine
            flow = -0.5 * flow
            p[at, rows] = visc[at, rows] * flow
            if is_own:
                u1_out[3, g, own] = flow
        return 0

    lax.fori_loop(0, SLABS, apply_first, 0)
    ghosts(d0, range(3))
    ghosts(p, [None])
    smooth()

    def apply_second(g, carry):
        at = g + 1
        lane = lane_index(8)
        y_at = lane & (EY - 1)
        x_at = (lane // EY) * SLABS + g
        own_cells = (x_at >= H) & (x_at < H + BX) & (y_at >= H) & (y_at < H + BY)
        acc = [jnp.zeros((8, LANES), jnp.float32) for _ in range(5)]
        for first, count in OWN_PIECES:
            rows = slice(first, first + count)
            here = slice(first - 8, first - 8 + count)
            own = slice(first - 16, first - 16 + count)
            centre = p[at, rows]
            press = (
                p[at - 1, rows],
                p[at + 1, rows],
                pltpu.roll(centre, 1, 1),
                pltpu.roll(centre, LANES - 1, 1),
                p[at, first - 1 : first - 1 + count],
                p[at, first + 1 : first + 1 + count],
            )
            flow = None
            values = []
            for c in range(3):
                mine, total, sides = neighbours(s, c, g, first, count)
                value = diag[g, here] * (mine - total) + 0.5 * (press[2 * c + 1] - press[2 * c])
                slope = sides[2 * c + 1] - sides[2 * c]
                flow = slope if flow is None else flow + slope
                s1_out[c, g, own] = mine
                values.append(value)
            values.append(-0.5 * flow)
            s1_out[3, g, own] = centre
            parts = [None] * 5
            for c in range(4):
                u2 = values[c]
                u2_out[c, g, own] = u2
                u1 = u1_out[c, g, own]
                pairs = [None, None, u1 * u1, u1 * u2, u2 * u2]
                if c < 3:
                    u0 = f[c, g, own]
                    pairs[0], pairs[1] = u0 * u1, u0 * u2
                for i, pair in enumerate(pairs):
                    if pair is not None:
                        parts[i] = pair if parts[i] is None else parts[i] + pair
            for i in range(5):
                acc[i] = acc[i] + (parts[i][:8] + parts[i][8:])
        return tuple(c + jnp.where(own_cells, a, 0.0) for c, a in zip(carry, acc))

    start = tuple(jnp.zeros((8, LANES), jnp.float32) for _ in range(5))
    acc = lax.fori_loop(0, SLABS, apply_second, start)
    lane = lane_index(1)
    line = jnp.zeros((1, LANES), jnp.float32)
    for i in range(5):
        both = jnp.sum(jnp.sum(acc[i], axis=0, keepdims=True), axis=1, keepdims=True)
        line = jnp.where(lane == i, both, line)
    sums[...] = line


def combine(gathered, f, s0, u1, s1, u2, solution_out, residual_out):
    line = jnp.sum(gathered[...], axis=0, keepdims=True)
    lane = lane_index(1)

    def entry(i):
        return jnp.sum(jnp.where(lane == i, line, 0.0), axis=1, keepdims=True)

    g01, g02, g11, g12, g22 = (entry(i) for i in range(5))
    lower = g12 / g11
    pivot = g22 - lower * g12
    b = (g02 - lower * g01) / pivot
    a = (g01 - g12 * b) / g11
    for g in range(SLABS):
        for c in range(4):
            if c < 3:
                sol = a * s0[c, g] + b * s1[c, g]
                res = f[c, g] - a * u1[c, g] - b * u2[c, g]
            else:
                sol = b * s1[c, g]
                res = -a * u1[c, g] - b * u2[c, g]
            for out, value in ((solution_out, sol), (residual_out, res)):
                back = value.T
                for k in range(CHUNKS):
                    x = k * SLABS + g - H
                    if 0 <= x < BX:
                        out[c, x] = back[k * EY + H : k * EY + H + BY]


def struct(*shape):
    return jax.ShapeDtypeStruct(shape, jnp.float32)


def call(kernel, outs, scratch=(), name=None):
    vmem = pl.BlockSpec(memory_space=pltpu.VMEM)

    def run(*args):
        return pl.pallas_call(
            kernel,
            out_shape=outs,
            in_specs=[vmem] * len(args),
            out_specs=[vmem] * len(outs),
            scratch_shapes=list(scratch),
            compiler_params=pltpu.CompilerParams(vmem_limit_bytes=60 * 1024 * 1024),
            name=name,
        )(*args)

    return run


def swap(tail, head, axis):
    count = lax.axis_size(axis)
    up = [(i, i + 1) for i in range(count - 1)]
    down = [(i + 1, i) for i in range(count - 1)]
    return lax.ppermute(tail, axis, up), lax.ppermute(head, axis, down)


def shards(viscosity, force):
    tail = jnp.concatenate([force[:, BX - 8 :].reshape(24, BY, BZ), viscosity[BX - 9 :]], axis=0)
    head = jnp.concatenate([force[:, :8].reshape(24, BY, BZ), viscosity[:9]], axis=0)
    low_x, high_x = swap(tail, head, "gx")
    tail, head = call(pack_y, [struct(YTILES, 8, BZ)] * 2, name="pack_y")(
        force, viscosity, low_x, high_x
    )
    low_y, high_y = swap(tail, head, "gy")
    field = (SLABS, BZ, LANES)
    f, v, ry, ex, tail, head = call(
        to_lanes,
        [struct(3, *field), struct(*field), struct(*field), struct(BZ, LANES)]
        + [struct(ZTILES, 8, LANES)] * 2,
        name="to_lanes",
    )(force, viscosity, low_x, high_x, low_y, high_y)
    low_z, high_z = swap(tail, head, "gz")
    ghosted = (SLABS + 2, ROWS, LANES)
    plain = (SLABS, EZ, LANES)
    shapes = [ghosted, (6, *plain), plain, plain] + [(3, *ghosted)] * 4 + [(3, *plain), ghosted]
    s0, u1, s1, u2, sums = call(
        solve_local,
        [struct(3, *field), struct(4, *field), struct(4, *field), struct(4, *field), struct(1, LANES)],
        [pltpu.VMEM(shape, jnp.float32) for shape in shapes],
        name="solve_local",
    )(f, v, ry, ex, low_z, high_z)
    devices = lax.axis_size(AXES)
    rows = jnp.broadcast_to(sums[None], (devices, 1, LANES))
    gathered = lax.all_to_all(rows, AXES, 0, 0).reshape(devices, LANES)
    block = struct(4, BX, BY, BZ)
    return tuple(call(combine, [block, block], name="combine")(gathered, f, s0, u1, s1, u2))


def solution(mesh):
    return jax.shard_map(
        shards,
        mesh=mesh,
        in_specs=(P("gx", "gy", "gz"), P(None, "gx", "gy", "gz")),
        out_specs=(P(None, "gx", "gy", "gz"), P(None, "gx", "gy", "gz")),
        check_vma=False,
    )
```

time: 447 us -> 128 us (0.29); the launches traced: 440 us -> 128 us
  other arithmetic: 130 us -> 0.04 us
  blocking collectives: 131 us -> 26.2 us
  local copies, waits for them, and re-layouts: 74.2 us -> 4.97 us
  starting transfers between devices: 75.9 us -> 17.9 us
  Pallas kernels: 0 us -> 46.6 us
  waiting for transfers between devices: 17.1 us -> 31.5 us
  between operations: 11.2 us -> 0.71 us
    psum x12 -> x0, blocking collectives: 131 us -> none  [one_axis_at_a_time(): shard = lax.psum(shard, axis)]
    add x10 -> x0, other arithmetic: 72.5 us -> none  [the longest x4 54.4 us: chebyshev(): ratio_next * ratio_now * update]
    ppermute x30 -> x6, starting transfers between devices: 75.9 us -> 17.9 us  [swap(): return (lax.ppermute(tail, axis, up), lax.ppermute(head, axis, down))]
    pallas_call x0 -> x4, Pallas kernels: none -> 46.6 us  [run(): pl.pallas_call(kernel, out_shape=outs, in_specs=[vmem] * len(args), out_s...]
    slice x41 -> x2, local copies, waits for them, and re-layouts: 32.4 us -> 1.99 us  [the longest x1 1.05 us: shards(): force[:, :8].reshape(24, BY, BZ)]
    all_to_all x0 -> x1, blocking collectives: none -> 26.2 us  [shards(): gathered = lax.all_to_all(rows, AXES, 0, 0).reshape(devices, LANES)]
    sub x2 -> x0, other arithmetic: 22.1 us -> none  [viscous(): result - y_plus * padded[:, 1:-1, 2:, 1:-1]]
    ppermute x12 -> x0, local copies, waits for them, and re-layouts: 15.6 us -> none  [the longest x4 5.19 us: extended(): lax.ppermute(head, axis, [((i + 1) % count, i) for i in range(ends)])]
  transfers between devices with their start and end apart: 30 -> 6, of which waited for: 8 -> 6; matrix products, arithmetic and copies ran while one was open for 12% -> 0% of each run, Pallas kernels for 0% -> 0%
where the time goes in v1:
time: 128 us
  Pallas kernels  46.6 us (36%)
  waiting for transfers between devices  31.5 us (25%)
  blocking collectives  26.2 us (20%)
  starting transfers between devices  17.9 us (14%)
  local copies, waits for them, and re-layouts  4.97 us (4%)
    pallas_call x4, Pallas kernels, run(): pl.pallas_call(kernel, out_shape=outs, in_specs=[vmem] * len(args), out_s...  46.6 us
    ppermute x6, waiting for transfers between devices, swap(): return (lax.ppermute(tail, axis, up), lax.ppermute(head, axis, down))  31.5 us
    all_to_all x1, blocking collectives, shards(): gathered = lax.all_to_all(rows, AXES, 0, 0).reshape(devices, LANES)  26.2 us
    ppermute x6, starting transfers between devices, swap(): return (lax.ppermute(tail, axis, up), lax.ppermute(head, axis, down))  17.9 us
  transfers between devices with their start and end apart: 6, of which 6 were waited for; matrix products, arithmetic and copies ran while one was open for 0% of the time, Pallas kernels for 0%

profile of v1, /device:TPU:1, one launch (start us, length us, event | category | flops | bytes accessed | tf_op | source)
XLA Modules:
  0.0 127.9 jit_solution(13753026718308041518)
XLA Ops:
  0.6 0.9 fusion.1
  1.6 1.1 fusion
  2.7 3.9 %collective-permute-start = (f32[33,16,128]{2,1,0:T(8,128)S(1)}, f32[33,16,128]{2,1,0:T(8,128)S(1)}, u32[]{:S(2)}, u32[]{:S(2)}) collective-permute-start(f32[33,16,128]{2,1,0:T(8,128)S(1)} %pad_maximum_fusion), channel_id=1, source_target_pairs={{0,64},{64,128},{128,192},{1,65},{65,129},{129,193},{2,66},{66,130... | collective-permute-start | bytes 811016 | tf_op jit(solution)/shard_map/ppermute | solution.py:379
  6.6 1.3 %collective-permute-start.1 = (f32[33,16,128]{2,1,0:T(8,128)S(1)}, f32[33,16,128]{2,1,0:T(8,128)S(1)}, u32[]{:S(2)}, u32[]{:S(2)}) collective-permute-start(f32[33,16,128]{2,1,0:T(8,128)S(1)} %pad_maximum_fusion.1), channel_id=1, source_target_pairs={{64,0},{128,64},{192,128},{65,1},{129,65},{193,129},{66,2},{130,66... | collective-permute-start | bytes 811016 | tf_op jit(solution)/shard_map/ppermute | solution.py:379
  7.9 3.8 %collective-permute-done.low_x = f32[33,16,128]{2,1,0:T(8,128)S(1)} collective-permute-done((f32[33,16,128]{2,1,0:T(8,128)S(1)}, f32[33,16,128]{2,1,0:T(8,128)S(1)}, u32[]{:S(2)}, u32[]{:S(2)}) %collective-permute-start) | collective-permute-done | bytes 270368 | tf_op jit(solution)/shard_map/ppermute | solution.py:379
  11.7 3.9 %collective-permute-done.1.high_x = f32[33,16,128]{2,1,0:T(8,128)S(1)} collective-permute-done((f32[33,16,128]{2,1,0:T(8,128)S(1)}, f32[33,16,128]{2,1,0:T(8,128)S(1)}, u32[]{:S(2)}, u32[]{:S(2)}) %collective-permute-start.1) | collective-permute-done | bytes 270368 | tf_op jit(solution)/shard_map/ppermute | solution.py:379
  15.6 0.0 copy-done
  15.6 0.7 copy-done.1
  16.3 2.6 %pack_y.1 = (f32[196,8,128]{2,1,0:T(8,128)}, f32[196,8,128]{2,1,0:T(8,128)}) custom-call(f32[3,32,16,128]{3,2,1,0:T(8,128)} %force.3, f32[32,16,128]{2,1,0:T(8,128)} %visc.3, f32[33,16,128]{2,1,0:T(8,128)} %copy-done, f32[33,16,128]{2,1,0:T(8,128)} %copy-done.1), custom_call_target="tpu_custom_call" | custom-call | tf_op jit(solution)/shard_map/pack_y/pallas_call | solution.py:362
  18.9 3.6 %collective-permute-start.2 = (f32[196,8,128]{2,1,0:T(8,128)}, f32[196,8,128]{2,1,0:T(8,128)S(1)}, u32[]{:S(2)}, u32[]{:S(2)}) collective-permute-start(f32[196,8,128]{2,1,0:T(8,128)} %get-tuple-element.15), channel_id=1, source_target_pairs={{0,8},{8,16},{16,24},{24,32},{32,40},{40,48},{48,56},{1,9},{9,17},... | collective-permute-start | bytes 2408456 | tf_op jit(solution)/shard_map/ppermute | solution.py:379
  22.5 1.3 %collective-permute-start.3 = (f32[196,8,128]{2,1,0:T(8,128)}, f32[196,8,128]{2,1,0:T(8,128)S(1)}, u32[]{:S(2)}, u32[]{:S(2)}) collective-permute-start(f32[196,8,128]{2,1,0:T(8,128)} %get-tuple-element.16), channel_id=1, source_target_pairs={{8,0},{16,8},{24,16},{32,24},{40,32},{48,40},{56,48},{9,1},{17,9},... | collective-permute-start | bytes 2408456 | tf_op jit(solution)/shard_map/ppermute | solution.py:379
  23.8 14.4 %collective-permute-done.2.low_y = f32[196,8,128]{2,1,0:T(8,128)S(1)} collective-permute-done((f32[196,8,128]{2,1,0:T(8,128)}, f32[196,8,128]{2,1,0:T(8,128)S(1)}, u32[]{:S(2)}, u32[]{:S(2)}) %collective-permute-start.2) | collective-permute-done | bytes 802848 | tf_op jit(solution)/shard_map/ppermute | solution.py:379
  38.2 4.0 %collective-permute-done.3.high_y = f32[196,8,128]{2,1,0:T(8,128)S(1)} collective-permute-done((f32[196,8,128]{2,1,0:T(8,128)}, f32[196,8,128]{2,1,0:T(8,128)S(1)}, u32[]{:S(2)}, u32[]{:S(2)}) %collective-permute-start.3) | collective-permute-done | bytes 802848 | tf_op jit(solution)/shard_map/ppermute | solution.py:379
  42.2 0.9 copy-done.3
  43.1 4.6 %to_lanes.1 = (f32[3,12,128,128]{3,2,1,0:T(8,128)}, f32[12,128,128]{2,1,0:T(8,128)}, f32[12,128,128]{2,1,0:T(8,128)}, f32[128,128]{1,0:T(8,128)}, f32[50,8,128]{2,1,0:T(8,128)}, /*index=5*/f32[50,8,128]{2,1,0:T(8,128)}) custom-call(f32[3,32,16,128]{3,2,1,0:T(8,128)} %force.3, f32[32,16,128]{2,1,0:T(8,128)} %visc.3, f32[33,16,128]{2,1,0:T(8,128)} %copy-done, ...), custom_call_target="tpu_custom_call" | custom-call | tf_op jit(solution)/shard_map/to_lanes/pallas_call | solution.py:362
  47.7 5.9 %collective-permute-start.4 = (f32[50,8,128]{2,1,0:T(8,128)}, f32[50,8,128]{2,1,0:T(8,128)S(1)}, u32[]{:S(2)}, u32[]{:S(2)}) collective-permute-start(f32[50,8,128]{2,1,0:T(8,128)} %get-tuple-element.21), channel_id=1, source_target_pairs={{0,1},{1,2},{2,3},{3,4},{4,5},{5,6},{6,7},{8,9},{9,10},{10,11},{11... | collective-permute-start | bytes 614408 | tf_op jit(solution)/shard_map/ppermute | solution.py:379
  53.6 1.9 %collective-permute-start.5 = (f32[50,8,128]{2,1,0:T(8,128)}, f32[50,8,128]{2,1,0:T(8,128)S(1)}, u32[]{:S(2)}, u32[]{:S(2)}) collective-permute-start(f32[50,8,128]{2,1,0:T(8,128)} %get-tuple-element.22), channel_id=1, source_target_pairs={{1,0},{2,1},{3,2},{4,3},{5,4},{6,5},{7,6},{9,8},{10,9},{11,10},{12... | collective-permute-start | bytes 614408 | tf_op jit(solution)/shard_map/ppermute | solution.py:379
  55.5 1.1 collective-permute-done.4.low_z
  56.6 4.3 %collective-permute-done.5.high_z = f32[50,8,128]{2,1,0:T(8,128)S(1)} collective-permute-done((f32[50,8,128]{2,1,0:T(8,128)}, f32[50,8,128]{2,1,0:T(8,128)S(1)}, u32[]{:S(2)}, u32[]{:S(2)}) %collective-permute-start.5) | collective-permute-done | bytes 204832 | tf_op jit(solution)/shard_map/ppermute | solution.py:379
  60.9 0.7 copy-done.5
  61.6 31.1 %solve_local.1 = (f32[3,12,128,128]{3,2,1,0:T(8,128)}, f32[4,12,128,128]{3,2,1,0:T(8,128)}, f32[4,12,128,128]{3,2,1,0:T(8,128)}, f32[4,12,128,128]{3,2,1,0:T(8,128)}, f32[1,128]{1,0:T(1,128)}) custom-call(f32[3,12,128,128]{3,2,1,0:T(8,128)} %get-tuple-element.17.f, f32[12,128,128]{2,1,0:T(8,128)} %get-tuple-element.18.v, ...), custom_call_target="tpu_custom_call" | custom-call | tf_op jit(solution)/shard_map/solve_local/pallas_call | solution.py:362
  92.7 0.7 broadcast_in_dim.9
  93.4 26.2 %all_to_all.5 = f32[256,1,128]{2,1,0:T(1,128)} all-to-all(f32[256,1,128]{2,1,0:T(1,128)S(1)} %broadcast_in_dim.9), channel_id=1, replica_groups=mesh['gx'=4,'gy'=8,'gz'=8] {'gx','gy','gz'}, dimensions={0} | all-to-all | bytes 262144 | tf_op jit(solution)/shard_map/all_to_all | solution.py:409
  119.6 8.3 %combine.1 = (f32[4,32,16,128]{3,2,1,0:T(8,128)}, f32[4,32,16,128]{3,2,1,0:T(8,128)}) custom-call(f32[256,128]{1,0:T(8,128)} %bitcast.6, f32[3,12,128,128]{3,2,1,0:T(8,128)} %get-tuple-element.17.f, f32[3,12,128,128]{3,2,1,0:T(8,128)} %get-tuple-element.24.s0, f32[4,12,128,128]{3,2,1,0:T(8,128)} %get-tuple-element.25.u1, ...), custom_call_target="tpu_custom_call" | custom-call | tf_op jit(solution)/shard_map/combine/pallas_call | solution.py:362
  (10 shorter events, 0.1 us)
Async XLA Ops:
  2.7 9.1 %collective-permute-start = (f32[33,16,128]{2,1,0:T(8,128)S(1)}, f32[33,16,128]{2,1,0:T(8,128)S(1)}, u32[]{:S(2)}, u32[]{:S(2)}) collective-permute-start(f32[33,16,128]{2,1,0:T(8,128)S(1)} %pad_maximum_fusion), channel_id=1, source_target_pairs={{0,64},{64,128},{128,192},{1,65},{65,129},{129,193},{2,66},{66,130... | collective-permute-start | bytes 811016 | tf_op jit(solution)/shard_map/ppermute | solution.py:379
  6.6 9.0 %collective-permute-start.1 = (f32[33,16,128]{2,1,0:T(8,128)S(1)}, f32[33,16,128]{2,1,0:T(8,128)S(1)}, u32[]{:S(2)}, u32[]{:S(2)}) collective-permute-start(f32[33,16,128]{2,1,0:T(8,128)S(1)} %pad_maximum_fusion.1), channel_id=1, source_target_pairs={{64,0},{128,64},{192,128},{65,1},{129,65},{193,129},{66,2},{130,66... | collective-permute-start | bytes 811016 | tf_op jit(solution)/shard_map/ppermute | solution.py:379
  11.7 3.9 %copy-start = (f32[33,16,128]{2,1,0:T(8,128)}, f32[33,16,128]{2,1,0:T(8,128)S(1)}, u32[]{:S(2)}) copy-start(f32[33,16,128]{2,1,0:T(8,128)S(1)} %collective-permute-done.low_x) | copy-start | bytes 811012
  15.6 0.7 copy-start.1
  18.9 19.3 %collective-permute-start.2 = (f32[196,8,128]{2,1,0:T(8,128)}, f32[196,8,128]{2,1,0:T(8,128)S(1)}, u32[]{:S(2)}, u32[]{:S(2)}) collective-permute-start(f32[196,8,128]{2,1,0:T(8,128)} %get-tuple-element.15), channel_id=1, source_target_pairs={{0,8},{8,16},{16,24},{24,32},{32,40},{40,48},{48,56},{1,9},{9,17},... | collective-permute-start | bytes 2408456 | tf_op jit(solution)/shard_map/ppermute | solution.py:379
  22.5 19.7 %collective-permute-start.3 = (f32[196,8,128]{2,1,0:T(8,128)}, f32[196,8,128]{2,1,0:T(8,128)S(1)}, u32[]{:S(2)}, u32[]{:S(2)}) collective-permute-start(f32[196,8,128]{2,1,0:T(8,128)} %get-tuple-element.16), channel_id=1, source_target_pairs={{8,0},{16,8},{24,16},{32,24},{40,32},{48,40},{56,48},{9,1},{17,9},... | collective-permute-start | bytes 2408456 | tf_op jit(solution)/shard_map/ppermute | solution.py:379
  38.2 4.1 %copy-start.2 = (f32[196,8,128]{2,1,0:T(8,128)}, f32[196,8,128]{2,1,0:T(8,128)S(1)}, u32[]{:S(2)}) copy-start(f32[196,8,128]{2,1,0:T(8,128)S(1)} %collective-permute-done.2.low_y) | copy-start | bytes 2408452
  42.2 0.9 copy-start.3
  47.7 8.9 %collective-permute-start.4 = (f32[50,8,128]{2,1,0:T(8,128)}, f32[50,8,128]{2,1,0:T(8,128)S(1)}, u32[]{:S(2)}, u32[]{:S(2)}) collective-permute-start(f32[50,8,128]{2,1,0:T(8,128)} %get-tuple-element.21), channel_id=1, source_target_pairs={{0,1},{1,2},{2,3},{3,4},{4,5},{5,6},{6,7},{8,9},{9,10},{10,11},{11... | collective-permute-start | bytes 614408 | tf_op jit(solution)/shard_map/ppermute | solution.py:379
  53.6 7.3 %collective-permute-start.5 = (f32[50,8,128]{2,1,0:T(8,128)}, f32[50,8,128]{2,1,0:T(8,128)S(1)}, u32[]{:S(2)}, u32[]{:S(2)}) collective-permute-start(f32[50,8,128]{2,1,0:T(8,128)} %get-tuple-element.22), channel_id=1, source_target_pairs={{1,0},{2,1},{3,2},{4,3},{5,4},{6,5},{7,6},{9,8},{10,9},{11,10},{12... | collective-permute-start | bytes 614408 | tf_op jit(solution)/shard_map/ppermute | solution.py:379
  56.6 4.3 %copy-start.4 = (f32[50,8,128]{2,1,0:T(8,128)}, f32[50,8,128]{2,1,0:T(8,128)S(1)}, u32[]{:S(2)}) copy-start(f32[50,8,128]{2,1,0:T(8,128)S(1)} %collective-permute-done.4.low_z) | copy-start | bytes 614404
  60.9 0.7 copy-start.5

commit v2 on v1

--- a/solution.py
+++ b/solution.py
@@ -17,54 +17,148 @@
 BX, BY, BZ, H = 32, 16, 128, 8
 EX, EY, EZ = BX + 2 * H, BY + 2 * H, BZ + 2 * H
 CHUNKS = 4
+UNROLL = 2
 SLABS = EX // CHUNKS
 LANES = CHUNKS * EY
 ROWS = EZ + 16
-YTILES = 4 * EX + BX // 8
 ZTILES = 4 * SLABS + 2
 OWN = slice(16, 16 + BZ)
 PIECES = [(8, 8)] + [(16 + 16 * i, 16) for i in range(8)] + [(144, 8)]
 OWN_PIECES = PIECES[1:-1]
 
 
-def chebyshev_factors():
+def smoother_polynomial():
+    def minus_operator(p):
+        return [high - low for low, high in zip(p + [0.0], [0.0] + p)]
+
+    def plus(p, q):
+        size = max(len(p), len(q))
+        return [x + y for x, y in zip(p + [0.0] * (size - len(p)), q + [0.0] * (size - len(q)))]
+
     scaled = MIDDLE / HALF
     now = 1.0 / scaled
-    pairs = []
+    update, remainder = [1.0 / MIDDLE], [1.0]
+    result = update
     for _ in range(CHEB - 1):
+        remainder = plus(remainder, minus_operator(update))
         following = 1.0 / (2.0 * scaled - now)
-        pairs.append((following * now, 2.0 * following / HALF))
+        update = plus(
+            [following * now * x for x in update], [2.0 * following / HALF * x for x in remainder]
+        )
+        result = plus(result, update)
         now = following
-    return pairs
+    return result
+
+
+def shared_tiles(reach):
+    def at(side, far):
+        return H - far if side == 0 else H + BX - 1 + far
+
+    tiles = []
+    for side in (0, 1):
+        for far in range(1, H + 1):
+            rows, other = reach - far, 2 * reach - 8 - far
+            if rows == 8 or far < other:
+                tiles.append((at(side, far), rows, None if rows == 8 else at(side, other)))
+    half = reach - 4
+    tiles.append((at(0, half), 4, at(1, half)))
+    return tiles
+
+
+FORCE_TILES = shared_tiles(8)
+VISC_TILES = shared_tiles(9)
+FORCE_COUNT = BX + len(FORCE_TILES)
+VISC_COUNT = BX + len(VISC_TILES)
+NINTH = 3 * FORCE_COUNT + VISC_COUNT
+YTILES = NINTH + BX // 8
+
+
+def tile_places(c):
+    base = c * FORCE_COUNT
+    places = {H + x: (base + x, None, False) for x in range(BX)}
+    for i, (first, rows, second) in enumerate(FORCE_TILES if c < 3 else VISC_TILES):
+        places[first] = (base + BX + i, rows, False)
+        if second is not None:
+            places[second] = (base + BX + i, rows, True)
+    return places
+
+
+def kept_if(condition, value):
+    return jnp.where(condition, value, 0.0)
+
+
+def at_start(axis):
+    return lax.axis_index(axis) == 0
+
+
+def at_end(axis):
+    return lax.axis_index(axis) == lax.axis_size(axis) - 1
+
+
+def pack_x(force, visc, force_out, visc_out, tail, head):
+    force_out[...] = force[...]
+    visc_out[...] = visc[...]
+    for c in range(3):
+        tail[c * 8 : c * 8 + 8] = force[c, BX - 8 :]
+        head[c * 8 : c * 8 + 8] = force[c, :8]
+    tail[24:] = visc[BX - 9 :]
+    head[24:] = visc[:9]
 
 
 def pack_y(force, visc, low_x, high_x, tail, head):
-    for out, first in ((tail, BY - 8), (head, 0)):
+    row = lax.broadcasted_iota(jnp.int32, (8, BZ), 0)
+    from_below, from_above = ~at_start("gx"), ~at_end("gx")
+    for out, up in ((tail, True), (head, False)):
+        first = BY - 8 if up else 0
         rows = slice(first, first + 8)
-        for c in range(3):
-            base = c * EX
-            out[base : base + 8] = low_x[c * 8 : c * 8 + 8, rows, :]
-            out[base + 8 : base + 8 + BX] = force[c, :, rows, :]
-            out[base + 8 + BX : base + EX] = high_x[c * 8 : c * 8 + 8, rows, :]
-        base = 3 * EX
-        out[base : base + 8] = low_x[25:33, rows, :]
-        out[base + 8 : base + 8 + BX] = visc[:, rows, :]
-        out[base + 8 + BX : base + EX] = high_x[24:32, rows, :]
-        ninth = first - 1 if first else 8
+
+        def tile(c, at):
+            if at < H:
+                if c < 3:
+                    return low_x[c * 8 + at, rows, :]
+                return kept_if(from_below, low_x[25 + at, rows, :])
+            at = at - H - BX
+            return high_x[c * 8 + at, rows, :] if c < 3 else kept_if(from_above, high_x[24 + at, rows, :])
+
+        for c in range(4):
+            base = c * FORCE_COUNT
+            out[base : base + BX] = force[c, :, rows, :] if c < 3 else visc[:, rows, :]
+            for i, (one, count, two) in enumerate(FORCE_TILES if c < 3 else VISC_TILES):
+                value = tile(c, one)
+                if two is not None:
+                    other = tile(c, two)
+                    if up:
+                        value = jnp.where(row >= 8 - count, value, pltpu.roll(other, 8 - count, 0))
+                    else:
+                        value = jnp.where(row < count, value, pltpu.roll(other, count, 0))
+                out[base + BX + i] = value
+        ninth = first - 1 if up else 8
         for x in range(BX):
-            out[4 * EX + x // 8, x % 8, :] = visc[x, ninth, :]
+            out[NINTH + x // 8, x % 8 : x % 8 + 1, :] = visc[x, ninth : ninth + 1, :]
 
 
 def to_lanes(force, visc, low_x, high_x, low_y, high_y, f_out, v_out, ry_out, ex_out, tail, head):
+    x_below, x_above = ~at_start("gx"), ~at_end("gx")
+    y_below, y_above = ~at_start("gy"), ~at_end("gy")
+    places = [tile_places(c) for c in range(4)]
+
     def rows_of(c, at):
         x = at - H
         if x < 0:
-            middle = low_x[c * 8 + at] if c < 3 else low_x[25 + at]
+            middle = low_x[c * 8 + at] if c < 3 else kept_if(x_below, low_x[25 + at])
         elif x >= BX:
-            middle = high_x[c * 8 + x - BX] if c < 3 else high_x[24 + x - BX]
+            middle = high_x[c * 8 + x - BX] if c < 3 else kept_if(x_above, high_x[24 + x - BX])
         else:
             middle = force[c, x] if c < 3 else visc[x]
-        return [low_y[c * EX + at], middle, high_y[c * EX + at]]
+        if at not in places[c]:
+            return [jnp.zeros((8, BZ), jnp.float32), middle, jnp.zeros((8, BZ), jnp.float32)]
+        where, count, second = places[c][at]
+        lower, upper = low_y[where], high_y[where]
+        if second:
+            lower, upper = pltpu.roll(lower, count, 0), pltpu.roll(upper, 8 - count, 0)
+        if c == 3:
+            lower, upper = kept_if(y_below, lower), kept_if(y_above, upper)
+        return [lower, middle, upper]
 
     for c in range(4):
         for g in range(SLABS):
@@ -88,8 +182,9 @@
         for k in range(CHUNKS):
             x = k * SLABS + g - H
             if 0 <= x < BX:
-                at = 4 * EX + x // 8
-                lower, upper = low_y[at, x % 8 : x % 8 + 1, :], high_y[at, x % 8 : x % 8 + 1, :]
+                at = NINTH + x // 8
+                lower = kept_if(y_below, low_y[at, x % 8 : x % 8 + 1, :])
+                upper = kept_if(y_above, high_y[at, x % 8 : x % 8 + 1, :])
             else:
                 lower = upper = jnp.zeros((1, BZ), jnp.float32)
             parts += [lower, nothing, upper]
@@ -97,7 +192,11 @@
     side = jnp.zeros((8, BZ), jnp.float32)
     between = jnp.zeros((2 * EY, BZ), jnp.float32)
     ex_out[...] = jnp.concatenate(
-        [side, low_x[24], side, between, side, high_x[32], side], axis=0
+        [
+            side, kept_if(x_below, low_x[24]), side, between,
+            side, kept_if(x_above, high_x[32]), side,
+        ],
+        axis=0,
     ).T
 
 
@@ -108,20 +207,25 @@
 def solve_local(
     f, v, ry, ex, low_z, high_z,
     s0_out, u1_out, s1_out, u2_out, sums,
-    visc, coef, inv, diag, d0, d1, d2, s, r, p,
+    visc, coef, inv, diag, d0, d1, d2, s, p,
 ):
+    z_below, z_above = ~at_start("gz"), ~at_end("gz")
+    *shape, leading = smoother_polynomial()
+    shape = [x / leading for x in shape]
+
     def place(g, _):
         visc[g + 1, 0:8] = jnp.zeros((8, LANES), jnp.float32)
         visc[g + 1, 152:160] = jnp.zeros((8, LANES), jnp.float32)
-        visc[g + 1, 8:16] = low_z[3 * SLABS + g]
+        visc[g + 1, 8:16] = kept_if(z_below, low_z[3 * SLABS + g])
         visc[g + 1, OWN] = v[g]
-        visc[g + 1, 144:152] = high_z[3 * SLABS + g]
+        visc[g + 1, 144:152] = kept_if(z_above, high_z[3 * SLABS + g])
         return 0
 
     lax.fori_loop(0, SLABS, place, 0)
     for g in range(SLABS):
-        visc[g + 1, 7:8] = low_z[4 * SLABS + g // 8, g % 8 : g % 8 + 1, :]
-        visc[g + 1, 152:153] = high_z[4 * SLABS + g // 8, g % 8 : g % 8 + 1, :]
+        ninth = (4 * SLABS + g // 8, slice(g % 8, g % 8 + 1))
+        visc[g + 1, 7:8] = kept_if(z_below, low_z[ninth])
+        visc[g + 1, 152:153] = kept_if(z_above, high_z[ninth])
     for first, count in PIECES:
         rows = slice(first, first + count)
         before = pltpu.roll(visc[SLABS, rows], EY, 1)
@@ -187,10 +291,10 @@
                     value = high_z[c * SLABS + g]
                 else:
                     value = f[c, g, first - 16 : first - 16 + count]
-                d0[c, at, rows] = value * inverse * (1.0 / MIDDLE)
+                d0[c, at, rows] = value * inverse * leading
         return 0
 
-    lax.fori_loop(0, SLABS, setup, 0)
+    lax.fori_loop(0, SLABS, setup, 0, unroll=UNROLL)
     ghosts(d0, range(3))
 
     def neighbours(ref, c, g, first, count):
@@ -208,33 +312,21 @@
         return mine, total, (x_minus, x_plus, below, above, z_minus, z_plus)
 
     def smooth():
-        factors = chebyshev_factors()
-        old = (d0, d1, d2)
+        chain = (d0, d1, d2, s)
         for step in range(CHEB - 1):
-            scale_d, scale_r = factors[step]
-            source = old[step]
-            last = step == CHEB - 2
+            source, target = chain[step], chain[step + 1]
+            weight = shape[CHEB - 2 - step]
 
             def body(g, _):
                 for first, count in PIECES:
                     rows = slice(first, first + count)
-                    here = slice(first - 8, first - 8 + count)
                     for c in range(3):
-                        mine, total, _ = neighbours(source, c, g, first, count)
-                        if step == 0:
-                            left = (MIDDLE - 1.0) * mine + total
-                        else:
-                            left = r[c, g, here] - mine + total
-                        new = scale_d * mine + scale_r * left
-                        if last:
-                            s[c, g + 1, rows] = d0[c, g + 1, rows] + d1[c, g + 1, rows] + mine + new
-                        else:
-                            r[c, g, here] = left
-                            old[step + 1][c, g + 1, rows] = new
+                        _, total, _ = neighbours(source, c, g, first, count)
+                        target[c, g + 1, rows] = total + weight * d0[c, g + 1, rows]
                 return 0
 
-            lax.fori_loop(0, SLABS, body, 0)
-            ghosts(s if last else old[step + 1], range(3))
+            lax.fori_loop(0, SLABS, body, 0, unroll=UNROLL)
+            ghosts(target, range(3))
 
     smooth()
 
@@ -251,7 +343,7 @@
                 value = diag[g, here] * (mine - total)
                 slope = sides[2 * c + 1] - sides[2 * c]
                 flow = slope if flow is None else flow + slope
-                d0[c, at, rows] = value * inv[g, here] * (1.0 / MIDDLE)
+                d0[c, at, rows] = value * inv[g, here] * leading
                 if is_own:
                     u1_out[c, g, own] = value
                     s0_out[c, g, own] = mine
@@ -261,7 +353,7 @@
                 u1_out[3, g, own] = flow
         return 0
 
-    lax.fori_loop(0, SLABS, apply_first, 0)
+    lax.fori_loop(0, SLABS, apply_first, 0, unroll=UNROLL)
     ghosts(d0, range(3))
     ghosts(p, [None])
     smooth()
@@ -314,7 +406,7 @@
         return tuple(c + jnp.where(own_cells, a, 0.0) for c, a in zip(carry, acc))
 
     start = tuple(jnp.zeros((8, LANES), jnp.float32) for _ in range(5))
-    acc = lax.fori_loop(0, SLABS, apply_second, start)
+    acc = lax.fori_loop(0, SLABS, apply_second, start, unroll=UNROLL)
     lane = lane_index(1)
     line = jnp.zeros((1, LANES), jnp.float32)
     for i in range(5):
@@ -355,7 +447,11 @@
     return jax.ShapeDtypeStruct(shape, jnp.float32)
 
 
-def call(kernel, outs, scratch=(), name=None):
+def kept(*shape):
+    return pltpu.VMEM(shape, jnp.float32)
+
+
+def call(kernel, outs, scratch=(), name=None, mib=16):
     vmem = pl.BlockSpec(memory_space=pltpu.VMEM)
 
     def run(*args):
@@ -365,7 +461,7 @@
             in_specs=[vmem] * len(args),
             out_specs=[vmem] * len(outs),
             scratch_shapes=list(scratch),
-            compiler_params=pltpu.CompilerParams(vmem_limit_bytes=60 * 1024 * 1024),
+            compiler_params=pltpu.CompilerParams(vmem_limit_bytes=mib * 1024 * 1024),
             name=name,
         )(*args)
 
@@ -374,35 +470,39 @@
 
 def swap(tail, head, axis):
     count = lax.axis_size(axis)
-    up = [(i, i + 1) for i in range(count - 1)]
-    down = [(i + 1, i) for i in range(count - 1)]
+    up = [(i, (i + 1) % count) for i in range(count)]
+    down = [(j, i) for i, j in up]
     return lax.ppermute(tail, axis, up), lax.ppermute(head, axis, down)
 
 
 def shards(viscosity, force):
-    tail = jnp.concatenate([force[:, BX - 8 :].reshape(24, BY, BZ), viscosity[BX - 9 :]], axis=0)
-    head = jnp.concatenate([force[:, :8].reshape(24, BY, BZ), viscosity[:9]], axis=0)
+    force, viscosity, tail, head = call(
+        pack_x,
+        [kept(3, BX, BY, BZ), kept(BX, BY, BZ)] + [kept(33, BY, BZ)] * 2,
+        name="pack_x",
+    )(force, viscosity)
     low_x, high_x = swap(tail, head, "gx")
-    tail, head = call(pack_y, [struct(YTILES, 8, BZ)] * 2, name="pack_y")(
+    tail, head = call(pack_y, [kept(YTILES, 8, BZ)] * 2, name="pack_y")(
         force, viscosity, low_x, high_x
     )
     low_y, high_y = swap(tail, head, "gy")
     field = (SLABS, BZ, LANES)
     f, v, ry, ex, tail, head = call(
         to_lanes,
-        [struct(3, *field), struct(*field), struct(*field), struct(BZ, LANES)]
-        + [struct(ZTILES, 8, LANES)] * 2,
+        [kept(3, *field), kept(*field), kept(*field), kept(BZ, LANES)]
+        + [kept(ZTILES, 8, LANES)] * 2,
         name="to_lanes",
     )(force, viscosity, low_x, high_x, low_y, high_y)
     low_z, high_z = swap(tail, head, "gz")
     ghosted = (SLABS + 2, ROWS, LANES)
     plain = (SLABS, EZ, LANES)
-    shapes = [ghosted, (6, *plain), plain, plain] + [(3, *ghosted)] * 4 + [(3, *plain), ghosted]
+    shapes = [ghosted, (6, *plain), plain, plain] + [(3, *ghosted)] * 4 + [ghosted]
     s0, u1, s1, u2, sums = call(
         solve_local,
-        [struct(3, *field), struct(4, *field), struct(4, *field), struct(4, *field), struct(1, LANES)],
+        [kept(3, *field), kept(4, *field), kept(4, *field), kept(4, *field), kept(1, LANES)],
         [pltpu.VMEM(shape, jnp.float32) for shape in shapes],
         name="solve_local",
+        mib=32,
     )(f, v, ry, ex, low_z, high_z)
     devices = lax.axis_size(AXES)
     rows = jnp.broadcast_to(sums[None], (devices, 1, LANES))

time: 128 us -> 87.4 us (0.68)
  Pallas kernels: 46.6 us -> 23.4 us
  waiting for transfers between devices: 31.5 us -> 24.3 us
  starting transfers between devices: 17.9 us -> 13.1 us
  local copies, waits for them, and re-layouts: 4.97 us -> 2.15 us
  blocking collectives: 26.2 us -> 23.7 us
    pallas_call x4 -> x5, Pallas kernels: 46.6 us -> 23.4 us  [run(): pl.pallas_call(kernel, out_shape=outs, in_specs=[vmem] * len(args), out_s...]
    ppermute x6, waiting for transfers between devices: 31.5 us -> 24.3 us  [swap(): return (lax.ppermute(tail, axis, up), lax.ppermute(head, axis, down))]
    ppermute x6, starting transfers between devices: 17.9 us -> 13.1 us  [swap(): return (lax.ppermute(tail, axis, up), lax.ppermute(head, axis, down))]
    all_to_all x1, blocking collectives: 26.2 us -> 23.7 us  [shards(): gathered = lax.all_to_all(rows, AXES, 0, 0).reshape(devices, LANES)]
    slice x2 -> x0, local copies, waits for them, and re-layouts: 1.99 us -> none  [the longest x1 1.05 us: shards(): force[:, :8].reshape(24, BY, BZ)]
  transfers between devices with their start and end apart: 6 -> 6, of which waited for: 6 -> 5; matrix products, arithmetic and copies ran while one was open for 0% -> 0% of each run, Pallas kernels for 0% -> 0%
where the time goes in v2:
time: 87.4 us; the launch traced here: 87.3 us
  waiting for transfers between devices  24.3 us (28%)
  blocking collectives  23.7 us (27%)
  Pallas kernels  23.4 us (27%)
  starting transfers between devices  13.1 us (15%)
  local copies, waits for them, and re-layouts  2.15 us (2%)
    ppermute x6, waiting for transfers between devices, swap(): return (lax.ppermute(tail, axis, up), lax.ppermute(head, axis, down))  24.3 us
    all_to_all x1, blocking collectives, shards(): gathered = lax.all_to_all(rows, AXES, 0, 0).reshape(devices, LANES)  23.7 us
    pallas_call x5, Pallas kernels, run(): pl.pallas_call(kernel, out_shape=outs, in_specs=[vmem] * len(args), out_s...  23.4 us
    ppermute x6, starting transfers between devices, swap(): return (lax.ppermute(tail, axis, up), lax.ppermute(head, axis, down))  13.1 us
    unnamed x4, local copies, waits for them, and re-layouts  2.08 us
  transfers between devices with their start and end apart: 6, of which 5 were waited for; matrix products, arithmetic and copies ran while one was open for 0% of the time, Pallas kernels for 0%

profile of v2, /device:TPU:1, one launch (start us, length us, event | category | flops | bytes accessed | tf_op | source)
XLA Modules:
  0.0 87.3 jit_solution(7369378992513675162)
XLA Ops:
  0.6 0.0 copy-start
  0.6 1.1 %copy-done = f32[3,32,16,128]{3,2,1,0:T(8,128)S(1)} copy-done((f32[3,32,16,128]{3,2,1,0:T(8,128)S(1)}, f32[3,32,16,128]{3,2,1,0:T(8,128)}, u32[]{:S(2)}) %copy-start) | copy-done | bytes 786456
  1.8 0.0 copy-start.1
  1.8 0.9 %copy-done.1 = f32[32,16,128]{2,1,0:T(8,128)S(1)} copy-done((f32[32,16,128]{2,1,0:T(8,128)S(1)}, f32[32,16,128]{2,1,0:T(8,128)}, u32[]{:S(2)}) %copy-start.1) | copy-done | bytes 262168
  2.7 0.1 pack_x.1
  2.8 2.1 %collective-permute-start = (f32[33,16,128]{2,1,0:T(8,128)S(1)}, f32[33,16,128]{2,1,0:T(8,128)S(1)}, u32[]{:S(2)}, u32[]{:S(2)}) collective-permute-start(f32[33,16,128]{2,1,0:T(8,128)S(1)} %get-tuple-element.21), channel_id=1, source_target_pairs={{0,64},{64,128},{128,192},{192,0},{1,65},{65,129},{129,193},{193,1... | collective-permute-start | bytes 811016 | tf_op jit(solution)/shard_map/ppermute | solution.py:475
  4.9 1.4 %collective-permute-start.1 = (f32[33,16,128]{2,1,0:T(8,128)S(1)}, f32[33,16,128]{2,1,0:T(8,128)S(1)}, u32[]{:S(2)}, u32[]{:S(2)}) collective-permute-start(f32[33,16,128]{2,1,0:T(8,128)S(1)} %get-tuple-element.22), channel_id=1, source_target_pairs={{64,0},{128,64},{192,128},{0,192},{65,1},{129,65},{193,129},{1,193... | collective-permute-start | bytes 811016 | tf_op jit(solution)/shard_map/ppermute | solution.py:475
  6.3 3.8 %collective-permute-done.low_x = f32[33,16,128]{2,1,0:T(8,128)S(1)} collective-permute-done((f32[33,16,128]{2,1,0:T(8,128)S(1)}, f32[33,16,128]{2,1,0:T(8,128)S(1)}, u32[]{:S(2)}, u32[]{:S(2)}) %collective-permute-start) | collective-permute-done | bytes 270368 | tf_op jit(solution)/shard_map/ppermute | solution.py:475
  10.0 1.7 %collective-permute-done.1.high_x = f32[33,16,128]{2,1,0:T(8,128)S(1)} collective-permute-done((f32[33,16,128]{2,1,0:T(8,128)S(1)}, f32[33,16,128]{2,1,0:T(8,128)S(1)}, u32[]{:S(2)}, u32[]{:S(2)}) %collective-permute-start.1) | collective-permute-done | bytes 270368 | tf_op jit(solution)/shard_map/ppermute | solution.py:475
  11.7 0.1 pack_y.1
  11.8 2.3 %collective-permute-start.2 = (f32[162,8,128]{2,1,0:T(8,128)S(1)}, f32[162,8,128]{2,1,0:T(8,128)S(1)}, u32[]{:S(2)}, u32[]{:S(2)}) collective-permute-start(f32[162,8,128]{2,1,0:T(8,128)S(1)} %get-tuple-element.23), channel_id=1, source_target_pairs={{0,8},{8,16},{16,24},{24,32},{32,40},{40,48},{48,56},{56,0},{1,9},... | collective-permute-start | bytes 1990664 | tf_op jit(solution)/shard_map/ppermute | solution.py:475
  14.1 4.0 %collective-permute-start.3 = (f32[162,8,128]{2,1,0:T(8,128)S(1)}, f32[162,8,128]{2,1,0:T(8,128)S(1)}, u32[]{:S(2)}, u32[]{:S(2)}) collective-permute-start(f32[162,8,128]{2,1,0:T(8,128)S(1)} %get-tuple-element.24), channel_id=1, source_target_pairs={{8,0},{16,8},{24,16},{32,24},{40,32},{48,40},{56,48},{0,56},{9,1},... | collective-permute-start | bytes 1990664 | tf_op jit(solution)/shard_map/ppermute | solution.py:475
  18.2 13.7 %collective-permute-done.2.low_y = f32[162,8,128]{2,1,0:T(8,128)S(1)} collective-permute-done((f32[162,8,128]{2,1,0:T(8,128)S(1)}, f32[162,8,128]{2,1,0:T(8,128)S(1)}, u32[]{:S(2)}, u32[]{:S(2)}) %collective-permute-start.2) | collective-permute-done | bytes 663584 | tf_op jit(solution)/shard_map/ppermute | solution.py:475
  31.8 0.0 collective-permute-done.3.high_y
  31.8 1.1 %to_lanes.1 = (f32[3,12,128,128]{3,2,1,0:T(8,128)S(1)}, f32[12,128,128]{2,1,0:T(8,128)S(1)}, f32[12,128,128]{2,1,0:T(8,128)S(1)}, f32[128,128]{1,0:T(8,128)S(1)}...) custom-call(f32[3,32,16,128]{3,2,1,0:T(8,128)S(1)} %get-tuple-element.19.force, ...), custom_call_target="tpu_custom_call" | custom-call | tf_op jit(solution)/shard_map/to_lanes/pallas_call | solution.py:458
  33.0 3.3 %collective-permute-start.4 = (f32[50,8,128]{2,1,0:T(8,128)S(1)}, f32[50,8,128]{2,1,0:T(8,128)S(1)}, u32[]{:S(2)}, u32[]{:S(2)}) collective-permute-start(f32[50,8,128]{2,1,0:T(8,128)S(1)} %get-tuple-element.29), channel_id=1, source_target_pairs={{0,1},{1,2},{2,3},{3,4},{4,5},{5,6},{6,7},{7,0},{8,9},{9,10},{10,1... | collective-permute-start | bytes 614408 | tf_op jit(solution)/shard_map/ppermute | solution.py:475
  36.3 0.0 collective-permute-start.5
  36.3 2.7 %collective-permute-done.4.low_z = f32[50,8,128]{2,1,0:T(8,128)S(1)} collective-permute-done((f32[50,8,128]{2,1,0:T(8,128)S(1)}, f32[50,8,128]{2,1,0:T(8,128)S(1)}, u32[]{:S(2)}, u32[]{:S(2)}) %collective-permute-start.4) | collective-permute-done | bytes 204832 | tf_op jit(solution)/shard_map/ppermute | solution.py:475
  39.0 2.5 %collective-permute-done.5.high_z = f32[50,8,128]{2,1,0:T(8,128)S(1)} collective-permute-done((f32[50,8,128]{2,1,0:T(8,128)S(1)}, f32[50,8,128]{2,1,0:T(8,128)S(1)}, u32[]{:S(2)}, u32[]{:S(2)}) %collective-permute-start.5) | collective-permute-done | bytes 204832 | tf_op jit(solution)/shard_map/ppermute | solution.py:475
  41.4 19.0 %solve_local.1 = (f32[3,12,128,128]{3,2,1,0:T(8,128)S(1)}, f32[4,12,128,128]{3,2,1,0:T(8,128)S(1)}, f32[4,12,128,128]{3,2,1,0:T(8,128)S(1)}, f32[4,12,128,128]{3,2,1,0:T(8,128)S(1)}, f32[1,128]{1,0:T(1,128)S(1)}) custom-call(f32[3,12,128,128]{3,2,1,0:T(8,128)S(1)} %get-tuple-element.25.f, f32[12,128,128]{2,1,0:T(8,128)S(1)} %get-tuple-element.26.v, ...), custom_call_target="tpu_custom_call" | custom-call | tf_op jit(solution)/shard_map/solve_local/pallas_call | solution.py:458
  60.4 0.1 broadcast_in_dim.9
  60.5 23.7 %all_to_all.5 = f32[256,1,128]{2,1,0:T(1,128)S(1)} all-to-all(f32[256,1,128]{2,1,0:T(1,128)S(1)} %broadcast_in_dim.9), channel_id=1, replica_groups=mesh['gx'=4,'gy'=8,'gz'=8] {'gx','gy','gz'}, dimensions={0} | all-to-all | bytes 262144 | tf_op jit(solution)/shard_map/all_to_all | solution.py:509
  84.1 3.1 %combine.1 = (f32[4,32,16,128]{3,2,1,0:T(8,128)}, f32[4,32,16,128]{3,2,1,0:T(8,128)}) custom-call(f32[256,128]{1,0:T(8,128)S(1)} %bitcast.2, f32[3,12,128,128]{3,2,1,0:T(8,128)S(1)} %get-tuple-element.25.f, f32[3,12,128,128]{3,2,1,0:T(8,128)S(1)} %get-tuple-element.32.s0, f32[4,12,128,128]{3,2,1,0:T(8,128)S(1)} %get-tuple-element.33.u1, ...), custom_call_target="tpu_custom_call" | custom-call | tf_op jit(solution)/shard_map/combine/pallas_call | solution.py:458
Async XLA Ops:
  0.6 1.1 %copy-start = (f32[3,32,16,128]{3,2,1,0:T(8,128)S(1)}, f32[3,32,16,128]{3,2,1,0:T(8,128)}, u32[]{:S(2)}) copy-start(f32[3,32,16,128]{3,2,1,0:T(8,128)} %force.1) | copy-start | bytes 2359300
  1.8 0.9 %copy-start.1 = (f32[32,16,128]{2,1,0:T(8,128)S(1)}, f32[32,16,128]{2,1,0:T(8,128)}, u32[]{:S(2)}) copy-start(f32[32,16,128]{2,1,0:T(8,128)} %visc.1) | copy-start | bytes 786436
  2.8 7.2 %collective-permute-start = (f32[33,16,128]{2,1,0:T(8,128)S(1)}, f32[33,16,128]{2,1,0:T(8,128)S(1)}, u32[]{:S(2)}, u32[]{:S(2)}) collective-permute-start(f32[33,16,128]{2,1,0:T(8,128)S(1)} %get-tuple-element.21), channel_id=1, source_target_pairs={{0,64},{64,128},{128,192},{192,0},{1,65},{65,129},{129,193},{193,1... | collective-permute-start | bytes 811016 | tf_op jit(solution)/shard_map/ppermute | solution.py:475
  4.9 6.8 %collective-permute-start.1 = (f32[33,16,128]{2,1,0:T(8,128)S(1)}, f32[33,16,128]{2,1,0:T(8,128)S(1)}, u32[]{:S(2)}, u32[]{:S(2)}) collective-permute-start(f32[33,16,128]{2,1,0:T(8,128)S(1)} %get-tuple-element.22), channel_id=1, source_target_pairs={{64,0},{128,64},{192,128},{0,192},{65,1},{129,65},{193,129},{1,193... | collective-permute-start | bytes 811016 | tf_op jit(solution)/shard_map/ppermute | solution.py:475
  11.8 20.0 %collective-permute-start.2 = (f32[162,8,128]{2,1,0:T(8,128)S(1)}, f32[162,8,128]{2,1,0:T(8,128)S(1)}, u32[]{:S(2)}, u32[]{:S(2)}) collective-permute-start(f32[162,8,128]{2,1,0:T(8,128)S(1)} %get-tuple-element.23), channel_id=1, source_target_pairs={{0,8},{8,16},{16,24},{24,32},{32,40},{40,48},{48,56},{56,0},{1,9},... | collective-permute-start | bytes 1990664 | tf_op jit(solution)/shard_map/ppermute | solution.py:475
  14.1 17.7 %collective-permute-start.3 = (f32[162,8,128]{2,1,0:T(8,128)S(1)}, f32[162,8,128]{2,1,0:T(8,128)S(1)}, u32[]{:S(2)}, u32[]{:S(2)}) collective-permute-start(f32[162,8,128]{2,1,0:T(8,128)S(1)} %get-tuple-element.24), channel_id=1, source_target_pairs={{8,0},{16,8},{24,16},{32,24},{40,32},{48,40},{56,48},{0,56},{9,1},... | collective-permute-start | bytes 1990664 | tf_op jit(solution)/shard_map/ppermute | solution.py:475
  33.0 6.0 %collective-permute-start.4 = (f32[50,8,128]{2,1,0:T(8,128)S(1)}, f32[50,8,128]{2,1,0:T(8,128)S(1)}, u32[]{:S(2)}, u32[]{:S(2)}) collective-permute-start(f32[50,8,128]{2,1,0:T(8,128)S(1)} %get-tuple-element.29), channel_id=1, source_target_pairs={{0,1},{1,2},{2,3},{3,4},{4,5},{5,6},{6,7},{7,0},{8,9},{9,10},{10,1... | collective-permute-start | bytes 614408 | tf_op jit(solution)/shard_map/ppermute | solution.py:475
  36.3 5.2 %collective-permute-start.5 = (f32[50,8,128]{2,1,0:T(8,128)S(1)}, f32[50,8,128]{2,1,0:T(8,128)S(1)}, u32[]{:S(2)}, u32[]{:S(2)}) collective-permute-start(f32[50,8,128]{2,1,0:T(8,128)S(1)} %get-tuple-element.30), channel_id=1, source_target_pairs={{1,0},{2,1},{3,2},{4,3},{5,4},{6,5},{7,6},{0,7},{9,8},{10,9},{11,1... | collective-permute-start | bytes 614408 | tf_op jit(solution)/shard_map/ppermute | solution.py:475

commit v3 on v2

--- a/solution.py
+++ b/solution.py
@@ -17,7 +17,7 @@
 BX, BY, BZ, H = 32, 16, 128, 8
 EX, EY, EZ = BX + 2 * H, BY + 2 * H, BZ + 2 * H
 CHUNKS = 4
-UNROLL = 2
+UNROLL = 4
 SLABS = EX // CHUNKS
 LANES = CHUNKS * EY
 ROWS = EZ + 16
@@ -67,19 +67,17 @@
 
 FORCE_TILES = shared_tiles(8)
 VISC_TILES = shared_tiles(9)
-FORCE_COUNT = BX + len(FORCE_TILES)
-VISC_COUNT = BX + len(VISC_TILES)
-NINTH = 3 * FORCE_COUNT + VISC_COUNT
-YTILES = NINTH + BX // 8
-
-
-def tile_places(c):
-    base = c * FORCE_COUNT
-    places = {H + x: (base + x, None, False) for x in range(BX)}
+FACE_TILES = 4 * BX + BX // 8
+CORNER_TILES = 3 * len(FORCE_TILES) + len(VISC_TILES)
+
+
+def corner_places(c):
+    places = {}
     for i, (first, rows, second) in enumerate(FORCE_TILES if c < 3 else VISC_TILES):
-        places[first] = (base + BX + i, rows, False)
+        at = c * len(FORCE_TILES) + i
+        places[first] = (at, rows, False)
         if second is not None:
-            places[second] = (base + BX + i, rows, True)
+            places[second] = (at, rows, True)
     return places
 
 
@@ -95,17 +93,29 @@
     return lax.axis_index(axis) == lax.axis_size(axis) - 1
 
 
-def pack_x(force, visc, force_out, visc_out, tail, head):
-    force_out[...] = force[...]
-    visc_out[...] = visc[...]
+def pack_faces(force_in, visc_in, force, visc, tail_x, head_x, tail_y, head_y, arrived):
+    copies = [
+        pltpu.make_async_copy(visc_in, visc, arrived.at[0]),
+        pltpu.make_async_copy(force_in, force, arrived.at[1]),
+    ]
+    for copy in copies:
+        copy.start()
+    copies[0].wait()
+    tail_x[24:] = visc[BX - 9 :]
+    head_x[24:] = visc[:9]
+    for out, first, ninth in ((tail_y, BY - 8, BY - 9), (head_y, 0, 8)):
+        out[3 * BX : 4 * BX] = visc[:, first : first + 8, :]
+        for x in range(BX):
+            out[4 * BX + x // 8, x % 8 : x % 8 + 1, :] = visc[x, ninth : ninth + 1, :]
+    copies[1].wait()
     for c in range(3):
-        tail[c * 8 : c * 8 + 8] = force[c, BX - 8 :]
-        head[c * 8 : c * 8 + 8] = force[c, :8]
-    tail[24:] = visc[BX - 9 :]
-    head[24:] = visc[:9]
-
-
-def pack_y(force, visc, low_x, high_x, tail, head):
+        tail_x[c * 8 : c * 8 + 8] = force[c, BX - 8 :]
+        head_x[c * 8 : c * 8 + 8] = force[c, :8]
+        tail_y[c * BX : c * BX + BX] = force[c, :, BY - 8 :, :]
+        head_y[c * BX : c * BX + BX] = force[c, :, :8, :]
+
+
+def pack_corners(low_x, high_x, tail, head):
     row = lax.broadcasted_iota(jnp.int32, (8, BZ), 0)
     from_below, from_above = ~at_start("gx"), ~at_end("gx")
     for out, up in ((tail, True), (head, False)):
@@ -121,8 +131,6 @@
             return high_x[c * 8 + at, rows, :] if c < 3 else kept_if(from_above, high_x[24 + at, rows, :])
 
         for c in range(4):
-            base = c * FORCE_COUNT
-            out[base : base + BX] = force[c, :, rows, :] if c < 3 else visc[:, rows, :]
             for i, (one, count, two) in enumerate(FORCE_TILES if c < 3 else VISC_TILES):
                 value = tile(c, one)
                 if two is not None:
@@ -131,16 +139,16 @@
                         value = jnp.where(row >= 8 - count, value, pltpu.roll(other, 8 - count, 0))
                     else:
                         value = jnp.where(row < count, value, pltpu.roll(other, count, 0))
-                out[base + BX + i] = value
-        ninth = first - 1 if up else 8
-        for x in range(BX):
-            out[NINTH + x // 8, x % 8 : x % 8 + 1, :] = visc[x, ninth : ninth + 1, :]
-
-
-def to_lanes(force, visc, low_x, high_x, low_y, high_y, f_out, v_out, ry_out, ex_out, tail, head):
+                out[c * len(FORCE_TILES) + i] = value
+
+
+def to_lanes(
+    force, visc, low_x, high_x, low_y, high_y, low_c, high_c,
+    f_out, v_out, ry_out, ex_out, tail, head,
+):
     x_below, x_above = ~at_start("gx"), ~at_end("gx")
     y_below, y_above = ~at_start("gy"), ~at_end("gy")
-    places = [tile_places(c) for c in range(4)]
+    places = [corner_places(c) for c in range(4)]
 
     def rows_of(c, at):
         x = at - H
@@ -150,12 +158,15 @@
             middle = high_x[c * 8 + x - BX] if c < 3 else kept_if(x_above, high_x[24 + x - BX])
         else:
             middle = force[c, x] if c < 3 else visc[x]
-        if at not in places[c]:
-            return [jnp.zeros((8, BZ), jnp.float32), middle, jnp.zeros((8, BZ), jnp.float32)]
-        where, count, second = places[c][at]
-        lower, upper = low_y[where], high_y[where]
-        if second:
-            lower, upper = pltpu.roll(lower, count, 0), pltpu.roll(upper, 8 - count, 0)
+        if 0 <= x < BX:
+            lower, upper = low_y[c * BX + x], high_y[c * BX + x]
+        elif at in places[c]:
+            where, count, second = places[c][at]
+            lower, upper = low_c[where], high_c[where]
+            if second:
+                lower, upper = pltpu.roll(lower, count, 0), pltpu.roll(upper, 8 - count, 0)
+        else:
+            lower = upper = jnp.zeros((8, BZ), jnp.float32)
         if c == 3:
             lower, upper = kept_if(y_below, lower), kept_if(y_above, upper)
         return [lower, middle, upper]
@@ -182,7 +193,7 @@
         for k in range(CHUNKS):
             x = k * SLABS + g - H
             if 0 <= x < BX:
-                at = NINTH + x // 8
+                at = 4 * BX + x // 8
                 lower = kept_if(y_below, low_y[at, x % 8 : x % 8 + 1, :])
                 upper = kept_if(y_above, high_y[at, x % 8 : x % 8 + 1, :])
             else:
@@ -451,14 +462,15 @@
     return pltpu.VMEM(shape, jnp.float32)
 
 
-def call(kernel, outs, scratch=(), name=None, mib=16):
+def call(kernel, outs, scratch=(), name=None, mib=16, source=pltpu.VMEM):
     vmem = pl.BlockSpec(memory_space=pltpu.VMEM)
+    given = pl.BlockSpec(memory_space=source)
 
     def run(*args):
         return pl.pallas_call(
             kernel,
             out_shape=outs,
-            in_specs=[vmem] * len(args),
+            in_specs=[given] * len(args),
             out_specs=[vmem] * len(outs),
             scratch_shapes=list(scratch),
             compiler_params=pltpu.CompilerParams(vmem_limit_bytes=mib * 1024 * 1024),
@@ -476,23 +488,28 @@
 
 
 def shards(viscosity, force):
-    force, viscosity, tail, head = call(
-        pack_x,
-        [kept(3, BX, BY, BZ), kept(BX, BY, BZ)] + [kept(33, BY, BZ)] * 2,
-        name="pack_x",
-    )(force, viscosity)
-    low_x, high_x = swap(tail, head, "gx")
-    tail, head = call(pack_y, [kept(YTILES, 8, BZ)] * 2, name="pack_y")(
-        force, viscosity, low_x, high_x
+    force, viscosity, tail_x, head_x, tail_y, head_y = call(
+        pack_faces,
+        [kept(3, BX, BY, BZ), kept(BX, BY, BZ)]
+        + [kept(33, BY, BZ)] * 2
+        + [kept(FACE_TILES, 8, BZ)] * 2,
+        [pltpu.SemaphoreType.DMA((2,))],
+        name="pack_faces",
+        source=pltpu.HBM,
+    )(*(pltpu.with_memory_space_constraint(x, pltpu.HBM) for x in (force, viscosity)))
+    low_y, high_y = swap(tail_y, head_y, "gy")
+    low_x, high_x = swap(tail_x, head_x, "gx")
+    tail, head = call(pack_corners, [kept(CORNER_TILES, 8, BZ)] * 2, name="pack_corners")(
+        low_x, high_x
     )
-    low_y, high_y = swap(tail, head, "gy")
+    low_c, high_c = swap(tail, head, "gy")
     field = (SLABS, BZ, LANES)
     f, v, ry, ex, tail, head = call(
         to_lanes,
         [kept(3, *field), kept(*field), kept(*field), kept(BZ, LANES)]
         + [kept(ZTILES, 8, LANES)] * 2,
         name="to_lanes",
-    )(force, viscosity, low_x, high_x, low_y, high_y)
+    )(force, viscosity, low_x, high_x, low_y, high_y, low_c, high_c)
     low_z, high_z = swap(tail, head, "gz")
     ghosted = (SLABS + 2, ROWS, LANES)
     plain = (SLABS, EZ, LANES)

time: 87.4 us -> 76.9 us (0.88)
  waiting for transfers between devices: 24.3 us -> 13.5 us
  starting transfers between devices: 13.1 us -> 15.7 us
  local copies, waits for them, and re-layouts: 2.15 us -> 0.07 us
    ppermute x6 -> x8, waiting for transfers between devices: 24.3 us -> 13.5 us  [swap(): return (lax.ppermute(tail, axis, up), lax.ppermute(head, axis, down))]
    ppermute x6 -> x8, starting transfers between devices: 13.1 us -> 15.7 us  [swap(): return (lax.ppermute(tail, axis, up), lax.ppermute(head, axis, down))]
    unnamed x4 -> x0, local copies, waits for them, and re-layouts: 2.08 us -> none
  transfers between devices with their start and end apart: 6 -> 8, of which waited for: 5 -> 4; matrix products, arithmetic and copies ran while one was open for 0% -> 0% of each run, Pallas kernels for 0% -> 0%
where the time goes in v3:
time: 76.9 us; the launch traced here: 76.7 us
  blocking collectives  24.1 us (31%)
  Pallas kernels  22.6 us (29%)
  starting transfers between devices  15.7 us (20%)
  waiting for transfers between devices  13.5 us (18%)
    all_to_all x1, blocking collectives, shards(): gathered = lax.all_to_all(rows, AXES, 0, 0).reshape(devices, LANES)  24.1 us
    pallas_call x5, Pallas kernels, run(): pl.pallas_call(kernel, out_shape=outs, in_specs=[given] * len(args), out_...  22.6 us
    ppermute x8, starting transfers between devices, swap(): return (lax.ppermute(tail, axis, up), lax.ppermute(head, axis, down))  15.7 us
    ppermute x8, waiting for transfers between devices, swap(): return (lax.ppermute(tail, axis, up), lax.ppermute(head, axis, down))  13.5 us
  transfers between devices with their start and end apart: 8, of which 4 were waited for; matrix products, arithmetic and copies ran while one was open for 0% of the time, Pallas kernels for 0%

profile of v3, /device:TPU:1, one launch (start us, length us, event | category | flops | bytes accessed | tf_op | source)
XLA Modules:
  0.0 76.7 jit_solution(12122377045011123449)
XLA Ops:
  0.6 1.3 %pack_faces.1 = (f32[3,32,16,128]{3,2,1,0:T(8,128)S(1)}, f32[32,16,128]{2,1,0:T(8,128)S(1)}, f32[33,16,128]{2,1,0:T(8,128)S(1)}, f32[33,16,128]{2,1,0:T(8,128)S(...) custom-call(f32[3,32,16,128]{3,2,1,0:T(8,128)} %force_in.1, f32[32,16,128]{2,1,0:T(8,128)} %visc_in.1), custom_call_target="tpu_custom_call" | custom-call | tf_op jit(solution)/shard_map/pack_faces/pallas_call | solution.py:470
  1.9 2.5 %collective-permute-start.2 = (f32[132,8,128]{2,1,0:T(8,128)S(1)}, f32[132,8,128]{2,1,0:T(8,128)S(1)}, u32[]{:S(2)}, u32[]{:S(2)}) collective-permute-start(f32[132,8,128]{2,1,0:T(8,128)S(1)} %get-tuple-element.25), channel_id=1, source_target_pairs={{0,8},{8,16},{16,24},{24,32},{32,40},{40,48},{48,56},{56,0},{1,9},... | collective-permute-start | bytes 1622024 | tf_op jit(solution)/shard_map/ppermute | solution.py:487
  4.5 4.0 %collective-permute-start.3 = (f32[132,8,128]{2,1,0:T(8,128)S(1)}, f32[132,8,128]{2,1,0:T(8,128)S(1)}, u32[]{:S(2)}, u32[]{:S(2)}) collective-permute-start(f32[132,8,128]{2,1,0:T(8,128)S(1)} %get-tuple-element.26), channel_id=1, source_target_pairs={{8,0},{16,8},{24,16},{32,24},{40,32},{48,40},{56,48},{0,56},{9,1},... | collective-permute-start | bytes 1622024 | tf_op jit(solution)/shard_map/ppermute | solution.py:487
  8.5 1.2 %collective-permute-start = (f32[33,16,128]{2,1,0:T(8,128)S(1)}, f32[33,16,128]{2,1,0:T(8,128)S(1)}, u32[]{:S(2)}, u32[]{:S(2)}) collective-permute-start(f32[33,16,128]{2,1,0:T(8,128)S(1)} %get-tuple-element.23), channel_id=1, source_target_pairs={{0,64},{64,128},{128,192},{192,0},{1,65},{65,129},{129,193},{193,1... | collective-permute-start | bytes 811016 | tf_op jit(solution)/shard_map/ppermute | solution.py:487
  9.7 1.5 %collective-permute-start.1 = (f32[33,16,128]{2,1,0:T(8,128)S(1)}, f32[33,16,128]{2,1,0:T(8,128)S(1)}, u32[]{:S(2)}, u32[]{:S(2)}) collective-permute-start(f32[33,16,128]{2,1,0:T(8,128)S(1)} %get-tuple-element.24), channel_id=1, source_target_pairs={{64,0},{128,64},{192,128},{0,192},{65,1},{129,65},{193,129},{1,193... | collective-permute-start | bytes 811016 | tf_op jit(solution)/shard_map/ppermute | solution.py:487
  11.2 5.6 %collective-permute-done.low_x = f32[33,16,128]{2,1,0:T(8,128)S(1)} collective-permute-done((f32[33,16,128]{2,1,0:T(8,128)S(1)}, f32[33,16,128]{2,1,0:T(8,128)S(1)}, u32[]{:S(2)}, u32[]{:S(2)}) %collective-permute-start) | collective-permute-done | bytes 270368 | tf_op jit(solution)/shard_map/ppermute | solution.py:487
  16.8 0.0 collective-permute-done.1.high_x
  16.9 0.1 collective-permute-start.4
  16.9 2.7 %collective-permute-start.5 = (f32[30,8,128]{2,1,0:T(8,128)S(1)}, f32[30,8,128]{2,1,0:T(8,128)S(1)}, u32[]{:S(2)}, u32[]{:S(2)}) collective-permute-start(f32[30,8,128]{2,1,0:T(8,128)S(1)} %get-tuple-element.28), channel_id=1, source_target_pairs={{8,0},{16,8},{24,16},{32,24},{40,32},{48,40},{56,48},{0,56},{9,1},... | collective-permute-start | bytes 368648 | tf_op jit(solution)/shard_map/ppermute | solution.py:487
  19.6 2.7 %collective-permute-done.4.low_c = f32[30,8,128]{2,1,0:T(8,128)S(1)} collective-permute-done((f32[30,8,128]{2,1,0:T(8,128)S(1)}, f32[30,8,128]{2,1,0:T(8,128)S(1)}, u32[]{:S(2)}, u32[]{:S(2)}) %collective-permute-start.4) | collective-permute-done | bytes 122912 | tf_op jit(solution)/shard_map/ppermute | solution.py:487
  22.3 0.0 collective-permute-done.5.high_c
  22.3 0.0 collective-permute-done.2.low_y
  22.3 0.0 collective-permute-done.3.high_y
  22.3 1.1 %to_lanes.1 = (f32[3,12,128,128]{3,2,1,0:T(8,128)S(1)}, f32[12,128,128]{2,1,0:T(8,128)S(1)}, f32[12,128,128]{2,1,0:T(8,128)S(1)}, f32[128,128]{1,0:T(8,128)S(1)}...) custom-call(f32[3,32,16,128]{3,2,1,0:T(8,128)S(1)} %get-tuple-element.21.force, ...), custom_call_target="tpu_custom_call" | custom-call | tf_op jit(solution)/shard_map/to_lanes/pallas_call | solution.py:470
  23.4 3.7 %collective-permute-start.6 = (f32[50,8,128]{2,1,0:T(8,128)S(1)}, f32[50,8,128]{2,1,0:T(8,128)S(1)}, u32[]{:S(2)}, u32[]{:S(2)}) collective-permute-start(f32[50,8,128]{2,1,0:T(8,128)S(1)} %get-tuple-element.33), channel_id=1, source_target_pairs={{0,1},{1,2},{2,3},{3,4},{4,5},{5,6},{6,7},{7,0},{8,9},{9,10},{10,1... | collective-permute-start | bytes 614408 | tf_op jit(solution)/shard_map/ppermute | solution.py:487
  27.2 0.0 collective-permute-start.7
  27.2 2.7 %collective-permute-done.6.low_z = f32[50,8,128]{2,1,0:T(8,128)S(1)} collective-permute-done((f32[50,8,128]{2,1,0:T(8,128)S(1)}, f32[50,8,128]{2,1,0:T(8,128)S(1)}, u32[]{:S(2)}, u32[]{:S(2)}) %collective-permute-start.6) | collective-permute-done | bytes 204832 | tf_op jit(solution)/shard_map/ppermute | solution.py:487
  29.9 2.5 %collective-permute-done.7.high_z = f32[50,8,128]{2,1,0:T(8,128)S(1)} collective-permute-done((f32[50,8,128]{2,1,0:T(8,128)S(1)}, f32[50,8,128]{2,1,0:T(8,128)S(1)}, u32[]{:S(2)}, u32[]{:S(2)}) %collective-permute-start.7) | collective-permute-done | bytes 204832 | tf_op jit(solution)/shard_map/ppermute | solution.py:487
  32.3 17.1 %solve_local.1 = (f32[3,12,128,128]{3,2,1,0:T(8,128)S(1)}, f32[4,12,128,128]{3,2,1,0:T(8,128)S(1)}, f32[4,12,128,128]{3,2,1,0:T(8,128)S(1)}, f32[4,12,128,128]{3,2,1,0:T(8,128)S(1)}, f32[1,128]{1,0:T(1,128)S(1)}) custom-call(f32[3,12,128,128]{3,2,1,0:T(8,128)S(1)} %get-tuple-element.29.f, f32[12,128,128]{2,1,0:T(8,128)S(1)} %get-tuple-element.30.v, ...), custom_call_target="tpu_custom_call" | custom-call | tf_op jit(solution)/shard_map/solve_local/pallas_call | solution.py:470
  49.4 0.1 broadcast_in_dim.9
  49.5 24.1 %all_to_all.5 = f32[256,1,128]{2,1,0:T(1,128)S(1)} all-to-all(f32[256,1,128]{2,1,0:T(1,128)S(1)} %broadcast_in_dim.9), channel_id=1, replica_groups=mesh['gx'=4,'gy'=8,'gz'=8] {'gx','gy','gz'}, dimensions={0} | all-to-all | bytes 262144 | tf_op jit(solution)/shard_map/all_to_all | solution.py:526
  73.6 3.1 %combine.1 = (f32[4,32,16,128]{3,2,1,0:T(8,128)}, f32[4,32,16,128]{3,2,1,0:T(8,128)}) custom-call(f32[256,128]{1,0:T(8,128)S(1)} %bitcast.2, f32[3,12,128,128]{3,2,1,0:T(8,128)S(1)} %get-tuple-element.29.f, f32[3,12,128,128]{3,2,1,0:T(8,128)S(1)} %get-tuple-element.36.s0, f32[4,12,128,128]{3,2,1,0:T(8,128)S(1)} %get-tuple-element.37.u1, ...), custom_call_target="tpu_custom_call" | custom-call | tf_op jit(solution)/shard_map/combine/pallas_call | solution.py:470
  (1 shorter events, 0.0 us)
Async XLA Ops:
  1.9 20.3 %collective-permute-start.2 = (f32[132,8,128]{2,1,0:T(8,128)S(1)}, f32[132,8,128]{2,1,0:T(8,128)S(1)}, u32[]{:S(2)}, u32[]{:S(2)}) collective-permute-start(f32[132,8,128]{2,1,0:T(8,128)S(1)} %get-tuple-element.25), channel_id=1, source_target_pairs={{0,8},{8,16},{16,24},{24,32},{32,40},{40,48},{48,56},{56,0},{1,9},... | collective-permute-start | bytes 1622024 | tf_op jit(solution)/shard_map/ppermute | solution.py:487
  4.5 17.8 %collective-permute-start.3 = (f32[132,8,128]{2,1,0:T(8,128)S(1)}, f32[132,8,128]{2,1,0:T(8,128)S(1)}, u32[]{:S(2)}, u32[]{:S(2)}) collective-permute-start(f32[132,8,128]{2,1,0:T(8,128)S(1)} %get-tuple-element.26), channel_id=1, source_target_pairs={{8,0},{16,8},{24,16},{32,24},{40,32},{48,40},{56,48},{0,56},{9,1},... | collective-permute-start | bytes 1622024 | tf_op jit(solution)/shard_map/ppermute | solution.py:487
  8.5 8.3 %collective-permute-start = (f32[33,16,128]{2,1,0:T(8,128)S(1)}, f32[33,16,128]{2,1,0:T(8,128)S(1)}, u32[]{:S(2)}, u32[]{:S(2)}) collective-permute-start(f32[33,16,128]{2,1,0:T(8,128)S(1)} %get-tuple-element.23), channel_id=1, source_target_pairs={{0,64},{64,128},{128,192},{192,0},{1,65},{65,129},{129,193},{193,1... | collective-permute-start | bytes 811016 | tf_op jit(solution)/shard_map/ppermute | solution.py:487
  9.7 7.1 %collective-permute-start.1 = (f32[33,16,128]{2,1,0:T(8,128)S(1)}, f32[33,16,128]{2,1,0:T(8,128)S(1)}, u32[]{:S(2)}, u32[]{:S(2)}) collective-permute-start(f32[33,16,128]{2,1,0:T(8,128)S(1)} %get-tuple-element.24), channel_id=1, source_target_pairs={{64,0},{128,64},{192,128},{0,192},{65,1},{129,65},{193,129},{1,193... | collective-permute-start | bytes 811016 | tf_op jit(solution)/shard_map/ppermute | solution.py:487
  16.9 5.4 %collective-permute-start.4 = (f32[30,8,128]{2,1,0:T(8,128)S(1)}, f32[30,8,128]{2,1,0:T(8,128)S(1)}, u32[]{:S(2)}, u32[]{:S(2)}) collective-permute-start(f32[30,8,128]{2,1,0:T(8,128)S(1)} %get-tuple-element.27), channel_id=1, source_target_pairs={{0,8},{8,16},{16,24},{24,32},{32,40},{40,48},{48,56},{56,0},{1,9},... | collective-permute-start | bytes 368648 | tf_op jit(solution)/shard_map/ppermute | solution.py:487
  16.9 5.3 %collective-permute-start.5 = (f32[30,8,128]{2,1,0:T(8,128)S(1)}, f32[30,8,128]{2,1,0:T(8,128)S(1)}, u32[]{:S(2)}, u32[]{:S(2)}) collective-permute-start(f32[30,8,128]{2,1,0:T(8,128)S(1)} %get-tuple-element.28), channel_id=1, source_target_pairs={{8,0},{16,8},{24,16},{32,24},{40,32},{48,40},{56,48},{0,56},{9,1},... | collective-permute-start | bytes 368648 | tf_op jit(solution)/shard_map/ppermute | solution.py:487
  23.4 6.4 %collective-permute-start.6 = (f32[50,8,128]{2,1,0:T(8,128)S(1)}, f32[50,8,128]{2,1,0:T(8,128)S(1)}, u32[]{:S(2)}, u32[]{:S(2)}) collective-permute-start(f32[50,8,128]{2,1,0:T(8,128)S(1)} %get-tuple-element.33), channel_id=1, source_target_pairs={{0,1},{1,2},{2,3},{3,4},{4,5},{5,6},{6,7},{7,0},{8,9},{9,10},{10,1... | collective-permute-start | bytes 614408 | tf_op jit(solution)/shard_map/ppermute | solution.py:487
  27.2 5.2 %collective-permute-start.7 = (f32[50,8,128]{2,1,0:T(8,128)S(1)}, f32[50,8,128]{2,1,0:T(8,128)S(1)}, u32[]{:S(2)}, u32[]{:S(2)}) collective-permute-start(f32[50,8,128]{2,1,0:T(8,128)S(1)} %get-tuple-element.34), channel_id=1, source_target_pairs={{1,0},{2,1},{3,2},{4,3},{5,4},{6,5},{7,6},{0,7},{9,8},{10,9},{11,1... | collective-permute-start | bytes 614408 | tf_op jit(solution)/shard_map/ppermute | solution.py:487

commit v4 on v3

--- a/solution.py
+++ b/solution.py
@@ -17,7 +17,7 @@
 BX, BY, BZ, H = 32, 16, 128, 8
 EX, EY, EZ = BX + 2 * H, BY + 2 * H, BZ + 2 * H
 CHUNKS = 4
-UNROLL = 4
+UNROLL = 12
 SLABS = EX // CHUNKS
 LANES = CHUNKS * EY
 ROWS = EZ + 16
@@ -25,6 +25,7 @@
 OWN = slice(16, 16 + BZ)
 PIECES = [(8, 8)] + [(16 + 16 * i, 16) for i in range(8)] + [(144, 8)]
 OWN_PIECES = PIECES[1:-1]
+END_PIECES = [(8, 8), (16, 8), (136, 8), (144, 8)]
 
 
 def smoother_polynomial():
@@ -215,63 +216,19 @@
     return lax.broadcasted_iota(jnp.int32, (rows, LANES), 1)
 
 
-def solve_local(
-    f, v, ry, ex, low_z, high_z,
-    s0_out, u1_out, s1_out, u2_out, sums,
-    visc, coef, inv, diag, d0, d1, d2, s, p,
-):
-    z_below, z_above = ~at_start("gz"), ~at_end("gz")
-    *shape, leading = smoother_polynomial()
-    shape = [x / leading for x in shape]
-
-    def place(g, _):
-        visc[g + 1, 0:8] = jnp.zeros((8, LANES), jnp.float32)
-        visc[g + 1, 152:160] = jnp.zeros((8, LANES), jnp.float32)
-        visc[g + 1, 8:16] = kept_if(z_below, low_z[3 * SLABS + g])
-        visc[g + 1, OWN] = v[g]
-        visc[g + 1, 144:152] = kept_if(z_above, high_z[3 * SLABS + g])
-        return 0
-
-    lax.fori_loop(0, SLABS, place, 0)
-    for g in range(SLABS):
-        ninth = (4 * SLABS + g // 8, slice(g % 8, g % 8 + 1))
-        visc[g + 1, 7:8] = kept_if(z_below, low_z[ninth])
-        visc[g + 1, 152:153] = kept_if(z_above, high_z[ninth])
-    for first, count in PIECES:
-        rows = slice(first, first + count)
-        before = pltpu.roll(visc[SLABS, rows], EY, 1)
-        after = pltpu.roll(visc[1, rows], LANES - EY, 1)
-        if 16 <= first < 144:
-            lane = lane_index(count)
-            extra = ex[first - 16 : first - 16 + count]
-            before = jnp.where(lane < EY, extra, before)
-            after = jnp.where(lane >= LANES - EY, extra, after)
-        visc[0, rows] = before
-        visc[SLABS + 1, rows] = after
-
-    def border(ref, which):
-        zero = jnp.zeros((8, LANES), jnp.float32)
-        for c in which:
-            for g in range(SLABS):
-                at = (c, g + 1) if c is not None else (g + 1,)
-                ref[(*at, slice(0, 8))] = zero
-                ref[(*at, slice(152, 160))] = zero
-
-    for ref in (d0, d1, d2, s):
-        border(ref, range(3))
-    border(p, [None])
-
-    def ghosts(ref, which):
-        for c in which:
-            for first, count in PIECES:
-                rows = slice(first, first + count)
-                pre = (c,) if c is not None else ()
-                ref[(*pre, 0, rows)] = pltpu.roll(ref[(*pre, SLABS, rows)], EY, 1)
-                ref[(*pre, SLABS + 1, rows)] = pltpu.roll(ref[(*pre, 1, rows)], LANES - EY, 1)
-
-    def setup(g, _):
+def ghosts(ref, which, pieces):
+    for c in which:
+        for first, count in pieces:
+            rows = slice(first, first + count)
+            pre = (c,) if c is not None else ()
+            ref[(*pre, 0, rows)] = pltpu.roll(ref[(*pre, SLABS, rows)], EY, 1)
+            ref[(*pre, SLABS + 1, rows)] = pltpu.roll(ref[(*pre, 1, rows)], LANES - EY, 1)
+
+
+def set_up(f, ry, visc, coef, inv, diag, d0, halo, leading, pieces):
+    def body(g, _):
         at = g + 1
-        for first, count in PIECES:
+        for first, count in pieces:
             rows = slice(first, first + count)
             here = slice(first - 8, first - 8 + count)
             lane = lane_index(count)
@@ -297,49 +254,109 @@
                 coef[i, g, here] = face * inverse
             for c in range(3):
                 if first == 8:
-                    value = low_z[c * SLABS + g]
+                    value = halo[0][c * SLABS + g]
                 elif first == 144:
-                    value = high_z[c * SLABS + g]
+                    value = halo[1][c * SLABS + g]
                 else:
                     value = f[c, g, first - 16 : first - 16 + count]
                 d0[c, at, rows] = value * inverse * leading
         return 0
 
-    lax.fori_loop(0, SLABS, setup, 0, unroll=UNROLL)
-    ghosts(d0, range(3))
-
-    def neighbours(ref, c, g, first, count):
-        at = g + 1
+    lax.fori_loop(0, SLABS, body, 0, unroll=UNROLL)
+    ghosts(d0, range(3), pieces)
+
+
+def neighbours(coef, ref, c, g, first, count):
+    at = g + 1
+    rows = slice(first, first + count)
+    here = slice(first - 8, first - 8 + count)
+    mine = ref[c, at, rows]
+    below, above = pltpu.roll(mine, 1, 1), pltpu.roll(mine, LANES - 1, 1)
+    x_minus, x_plus = ref[c, at - 1, rows], ref[c, at + 1, rows]
+    z_minus = ref[c, at, first - 1 : first - 1 + count]
+    z_plus = ref[c, at, first + 1 : first + 1 + count]
+    total = coef[0, g, here] * x_minus + coef[1, g, here] * x_plus
+    total = total + (coef[2, g, here] * below + coef[3, g, here] * above)
+    total = total + (coef[4, g, here] * z_minus + coef[5, g, here] * z_plus)
+    return mine, total, (x_minus, x_plus, below, above, z_minus, z_plus)
+
+
+def smoother_step(coef, source, target, d0, weight, pieces):
+    def body(g, _):
+        for first, count in pieces:
+            rows = slice(first, first + count)
+            for c in range(3):
+                _, total, _ = neighbours(coef, source, c, g, first, count)
+                target[c, g + 1, rows] = total + weight * d0[c, g + 1, rows]
+        return 0
+
+    lax.fori_loop(0, SLABS, body, 0, unroll=UNROLL)
+    ghosts(target, range(3), pieces)
+
+
+def prepare(f, v, ry, ex, visc, coef, inv, diag, d0, d1, d2):
+    *shape, leading = smoother_polynomial()
+
+    def place(g, _):
+        visc[g + 1, OWN] = v[g]
+        return 0
+
+    lax.fori_loop(0, SLABS, place, 0)
+    for first, count in OWN_PIECES:
         rows = slice(first, first + count)
-        here = slice(first - 8, first - 8 + count)
-        mine = ref[c, at, rows]
-        below, above = pltpu.roll(mine, 1, 1), pltpu.roll(mine, LANES - 1, 1)
-        x_minus, x_plus = ref[c, at - 1, rows], ref[c, at + 1, rows]
-        z_minus = ref[c, at, first - 1 : first - 1 + count]
-        z_plus = ref[c, at, first + 1 : first + 1 + count]
-        total = coef[0, g, here] * x_minus + coef[1, g, here] * x_plus
-        total = total + (coef[2, g, here] * below + coef[3, g, here] * above)
-        total = total + (coef[4, g, here] * z_minus + coef[5, g, here] * z_plus)
-        return mine, total, (x_minus, x_plus, below, above, z_minus, z_plus)
+        lane = lane_index(count)
+        extra = ex[first - 16 : first - 16 + count]
+        before = pltpu.roll(visc[SLABS, rows], EY, 1)
+        after = pltpu.roll(visc[1, rows], LANES - EY, 1)
+        visc[0, rows] = jnp.where(lane < EY, extra, before)
+        visc[SLABS + 1, rows] = jnp.where(lane >= LANES - EY, extra, after)
+    set_up(f, ry, visc, coef, inv, diag, d0, None, leading, OWN_PIECES)
+    smoother_step(coef, d0, d1, d0, shape[-1] / leading, OWN_PIECES)
+    smoother_step(coef, d1, d2, d0, shape[-2] / leading, OWN_PIECES)
+
+
+def solve_local(f, ry, low_z, high_z, *refs):
+    kept_refs, refs = refs[7:14], refs[14:]
+    visc, coef, inv, diag, d0, d1, d2 = kept_refs
+    s0_out, u1_out, s1_out, u2_out, sums, s, p = refs
+    z_below, z_above = ~at_start("gz"), ~at_end("gz")
+    *shape, leading = smoother_polynomial()
+    weights = [x / leading for x in reversed(shape)]
+    zero = jnp.zeros((8, LANES), jnp.float32)
+
+    def place(g, _):
+        visc[g + 1, 0:8] = zero
+        visc[g + 1, 152:160] = zero
+        visc[g + 1, 8:16] = kept_if(z_below, low_z[3 * SLABS + g])
+        visc[g + 1, 144:152] = kept_if(z_above, high_z[3 * SLABS + g])
+        return 0
+
+    lax.fori_loop(0, SLABS, place, 0)
+    for g in range(SLABS):
+        ninth = (4 * SLABS + g // 8, slice(g % 8, g % 8 + 1))
+        visc[g + 1, 7:8] = kept_if(z_below, low_z[ninth])
+        visc[g + 1, 152:153] = kept_if(z_above, high_z[ninth])
+
+    def border(ref, which):
+        for c in which:
+            for g in range(SLABS):
+                at = (c, g + 1) if c is not None else (g + 1,)
+                ref[(*at, slice(0, 8))] = zero
+                ref[(*at, slice(152, 160))] = zero
+
+    for ref in (d0, d1, d2, s):
+        border(ref, range(3))
+    border(p, [None])
+    ghosts(visc, [None], [END_PIECES[0], END_PIECES[-1]])
+    set_up(f, ry, visc, coef, inv, diag, d0, (low_z, high_z), leading, END_PIECES)
+    smoother_step(coef, d0, d1, d0, weights[0], END_PIECES)
+    smoother_step(coef, d1, d2, d0, weights[1], END_PIECES)
+    smoother_step(coef, d2, s, d0, weights[2], PIECES)
 
     def smooth():
         chain = (d0, d1, d2, s)
         for step in range(CHEB - 1):
-            source, target = chain[step], chain[step + 1]
-            weight = shape[CHEB - 2 - step]
-
-            def body(g, _):
-                for first, count in PIECES:
-                    rows = slice(first, first + count)
-                    for c in range(3):
-                        _, total, _ = neighbours(source, c, g, first, count)
-                        target[c, g + 1, rows] = total + weight * d0[c, g + 1, rows]
-                return 0
-
-            lax.fori_loop(0, SLABS, body, 0, unroll=UNROLL)
-            ghosts(target, range(3))
-
-    smooth()
+            smoother_step(coef, chain[step], chain[step + 1], d0, weights[step], PIECES)
 
     def apply_first(g, _):
         at = g + 1
@@ -350,7 +367,7 @@
             is_own = 16 <= first < 144
             flow = None
             for c in range(3):
-                mine, total, sides = neighbours(s, c, g, first, count)
+                mine, total, sides = neighbours(coef, s, c, g, first, count)
                 value = diag[g, here] * (mine - total)
                 slope = sides[2 * c + 1] - sides[2 * c]
                 flow = slope if flow is None else flow + slope
@@ -365,8 +382,8 @@
         return 0
 
     lax.fori_loop(0, SLABS, apply_first, 0, unroll=UNROLL)
-    ghosts(d0, range(3))
-    ghosts(p, [None])
+    ghosts(d0, range(3), PIECES)
+    ghosts(p, [None], PIECES)
     smooth()
 
     def apply_second(g, carry):
@@ -392,7 +409,7 @@
             flow = None
             values = []
             for c in range(3):
-                mine, total, sides = neighbours(s, c, g, first, count)
+                mine, total, sides = neighbours(coef, s, c, g, first, count)
                 value = diag[g, here] * (mine - total) + 0.5 * (press[2 * c + 1] - press[2 * c])
                 slope = sides[2 * c + 1] - sides[2 * c]
                 flow = slope if flow is None else flow + slope
@@ -426,7 +443,7 @@
     sums[...] = line
 
 
-def combine(gathered, f, s0, u1, s1, u2, solution_out, residual_out):
+def combine(gathered, f, s0, u1, s1, u2, solution_to, residual_to, solution_out, residual_out, done):
     line = jnp.sum(gathered[...], axis=0, keepdims=True)
     lane = lane_index(1)
 
@@ -438,8 +455,9 @@
     pivot = g22 - lower * g12
     b = (g02 - lower * g01) / pivot
     a = (g01 - g12 * b) / g11
-    for g in range(SLABS):
-        for c in range(4):
+    copies = []
+    for c in range(4):
+        for g in range(SLABS):
             if c < 3:
                 sol = a * s0[c, g] + b * s1[c, g]
                 res = f[c, g] - a * u1[c, g] - b * u2[c, g]
@@ -452,6 +470,11 @@
                     x = k * SLABS + g - H
                     if 0 <= x < BX:
                         out[c, x] = back[k * EY + H : k * EY + H + BY]
+        for i, (out, to) in enumerate(((solution_out, solution_to), (residual_out, residual_to))):
+            copies.append(pltpu.make_async_copy(out.at[c], to.at[c], done.at[2 * c + i]))
+            copies[-1].start()
+    for copy in copies:
+        copy.wait()
 
 
 def struct(*shape):
@@ -462,8 +485,10 @@
     return pltpu.VMEM(shape, jnp.float32)
 
 
-def call(kernel, outs, scratch=(), name=None, mib=16, source=pltpu.VMEM):
-    vmem = pl.BlockSpec(memory_space=pltpu.VMEM)
+def call(
+    kernel, outs, scratch=(), name=None, mib=16, source=pltpu.VMEM, to=pltpu.VMEM, alias=None, flops=None
+):
+    result = pl.BlockSpec(memory_space=to)
     given = pl.BlockSpec(memory_space=source)
 
     def run(*args):
@@ -471,7 +496,9 @@
             kernel,
             out_shape=outs,
             in_specs=[given] * len(args),
-            out_specs=[vmem] * len(outs),
+            out_specs=[result] * len(outs),
+            input_output_aliases=alias or {},
+            cost_estimate=flops and pl.CostEstimate(flops=flops, bytes_accessed=0, transcendentals=0),
             scratch_shapes=list(scratch),
             compiler_params=pltpu.CompilerParams(vmem_limit_bytes=mib * 1024 * 1024),
             name=name,
@@ -513,19 +540,31 @@
     low_z, high_z = swap(tail, head, "gz")
     ghosted = (SLABS + 2, ROWS, LANES)
     plain = (SLABS, EZ, LANES)
-    shapes = [ghosted, (6, *plain), plain, plain] + [(3, *ghosted)] * 4 + [ghosted]
-    s0, u1, s1, u2, sums = call(
+    state_shapes = [kept(*ghosted), kept(6, *plain), kept(*plain), kept(*plain)]
+    state_shapes += [kept(3, *ghosted)] * 3
+    state = call(prepare, state_shapes, name="prepare", flops=120 * EX * EY * BZ)(f, v, ry, ex)
+    *_, s0, u1, s1, u2, sums = call(
         solve_local,
-        [kept(3, *field), kept(4, *field), kept(4, *field), kept(4, *field), kept(1, LANES)],
-        [pltpu.VMEM(shape, jnp.float32) for shape in shapes],
+        state_shapes
+        + [kept(3, *field), kept(4, *field), kept(4, *field), kept(4, *field), kept(1, LANES)],
+        [pltpu.VMEM((3, *ghosted), jnp.float32), pltpu.VMEM(ghosted, jnp.float32)],
         name="solve_local",
-        mib=32,
-    )(f, v, ry, ex, low_z, high_z)
+        alias={4 + i: i for i in range(7)},
+    )(f, ry, low_z, high_z, *state)
     devices = lax.axis_size(AXES)
     rows = jnp.broadcast_to(sums[None], (devices, 1, LANES))
     gathered = lax.all_to_all(rows, AXES, 0, 0).reshape(devices, LANES)
     block = struct(4, BX, BY, BZ)
-    return tuple(call(combine, [block, block], name="combine")(gathered, f, s0, u1, s1, u2))
+    whole = pltpu.VMEM((4, BX, BY, BZ), jnp.float32)
+    return tuple(
+        call(
+            combine,
+            [block, block],
+            [whole, whole, pltpu.SemaphoreType.DMA((8,))],
+            name="combine",
+            to=pltpu.HBM,
+        )(gathered, f, s0, u1, s1, u2)
+    )
 
 
 def solution(mesh):

time: 76.9 us -> 74 us (0.962)
  waiting for transfers between devices: 13.5 us -> 9.12 us
  Pallas kernels: 22.6 us -> 24 us
    ppermute x8, waiting for transfers between devices: 13.5 us -> 9.12 us  [swap(): return (lax.ppermute(tail, axis, up), lax.ppermute(head, axis, down))]
    pallas_call x5 -> x6, Pallas kernels: 22.6 us -> 24 us  [run(): pl.pallas_call(kernel, out_shape=outs, in_specs=[given] * len(args), out_...]
  transfers between devices with their start and end apart: 8 -> 8, of which waited for: 4 -> 3; matrix products, arithmetic and copies ran while one was open for 0% -> 0% of each run, Pallas kernels for 0% -> 6%
where the time goes in v4:
time: 74 us; the launch traced here: 73.9 us
  blocking collectives  24.1 us (33%)
  Pallas kernels  24 us (32%)
  starting transfers between devices  15.7 us (21%)
  waiting for transfers between devices  9.12 us (12%)
  between operations  0.86 us (1%)
    all_to_all x1, blocking collectives, shards(): gathered = lax.all_to_all(rows, AXES, 0, 0).reshape(devices, LANES)  24.1 us
    pallas_call x6, Pallas kernels, run(): pl.pallas_call(kernel, out_shape=outs, in_specs=[given] * len(args), out_...  24 us
    ppermute x8, starting transfers between devices, swap(): return (lax.ppermute(tail, axis, up), lax.ppermute(head, axis, down))  15.7 us
    ppermute x8, waiting for transfers between devices, swap(): return (lax.ppermute(tail, axis, up), lax.ppermute(head, axis, down))  9.12 us
  transfers between devices with their start and end apart: 8, of which 3 were waited for; matrix products, arithmetic and copies ran while one was open for 0% of the time, Pallas kernels for 6%

profile of v4, /device:TPU:1, one launch (start us, length us, event | category | flops | bytes accessed | tf_op | source)
XLA Modules:
  0.0 73.9 jit_solution(16399336892673409636)
XLA Ops:
  0.6 1.3 %pack_faces.1 = (f32[3,32,16,128]{3,2,1,0:T(8,128)S(1)}, f32[32,16,128]{2,1,0:T(8,128)S(1)}, f32[33,16,128]{2,1,0:T(8,128)S(1)}, f32[33,16,128]{2,1,0:T(8,128)S(...) custom-call(f32[3,32,16,128]{3,2,1,0:T(8,128)} %force_in.1, f32[32,16,128]{2,1,0:T(8,128)} %visc_in.1), custom_call_target="tpu_custom_call" | custom-call | tf_op jit(solution)/shard_map/pack_faces/pallas_call | solution.py:495
  1.9 2.5 %collective-permute-start.2 = (f32[132,8,128]{2,1,0:T(8,128)S(1)}, f32[132,8,128]{2,1,0:T(8,128)S(1)}, u32[]{:S(2)}, u32[]{:S(2)}) collective-permute-start(f32[132,8,128]{2,1,0:T(8,128)S(1)} %get-tuple-element.32), channel_id=1, source_target_pairs={{0,8},{8,16},{16,24},{24,32},{32,40},{40,48},{48,56},{56,0},{1,9},... | collective-permute-start | bytes 1622024 | tf_op jit(solution)/shard_map/ppermute | solution.py:514
  4.5 4.0 %collective-permute-start.3 = (f32[132,8,128]{2,1,0:T(8,128)S(1)}, f32[132,8,128]{2,1,0:T(8,128)S(1)}, u32[]{:S(2)}, u32[]{:S(2)}) collective-permute-start(f32[132,8,128]{2,1,0:T(8,128)S(1)} %get-tuple-element.33), channel_id=1, source_target_pairs={{8,0},{16,8},{24,16},{32,24},{40,32},{48,40},{56,48},{0,56},{9,1},... | collective-permute-start | bytes 1622024 | tf_op jit(solution)/shard_map/ppermute | solution.py:514
  8.5 1.2 %collective-permute-start = (f32[33,16,128]{2,1,0:T(8,128)S(1)}, f32[33,16,128]{2,1,0:T(8,128)S(1)}, u32[]{:S(2)}, u32[]{:S(2)}) collective-permute-start(f32[33,16,128]{2,1,0:T(8,128)S(1)} %get-tuple-element.30), channel_id=1, source_target_pairs={{0,64},{64,128},{128,192},{192,0},{1,65},{65,129},{129,193},{193,1... | collective-permute-start | bytes 811016 | tf_op jit(solution)/shard_map/ppermute | solution.py:514
  9.7 1.5 %collective-permute-start.1 = (f32[33,16,128]{2,1,0:T(8,128)S(1)}, f32[33,16,128]{2,1,0:T(8,128)S(1)}, u32[]{:S(2)}, u32[]{:S(2)}) collective-permute-start(f32[33,16,128]{2,1,0:T(8,128)S(1)} %get-tuple-element.31), channel_id=1, source_target_pairs={{64,0},{128,64},{192,128},{0,192},{65,1},{129,65},{193,129},{1,193... | collective-permute-start | bytes 811016 | tf_op jit(solution)/shard_map/ppermute | solution.py:514
  11.2 5.6 %collective-permute-done.low_x = f32[33,16,128]{2,1,0:T(8,128)S(1)} collective-permute-done((f32[33,16,128]{2,1,0:T(8,128)S(1)}, f32[33,16,128]{2,1,0:T(8,128)S(1)}, u32[]{:S(2)}, u32[]{:S(2)}) %collective-permute-start) | collective-permute-done | bytes 270368 | tf_op jit(solution)/shard_map/ppermute | solution.py:514
  16.8 0.0 collective-permute-done.1.high_x
  16.9 0.1 collective-permute-start.4
  16.9 2.7 %collective-permute-start.5 = (f32[30,8,128]{2,1,0:T(8,128)S(1)}, f32[30,8,128]{2,1,0:T(8,128)S(1)}, u32[]{:S(2)}, u32[]{:S(2)}) collective-permute-start(f32[30,8,128]{2,1,0:T(8,128)S(1)} %get-tuple-element.35), channel_id=1, source_target_pairs={{8,0},{16,8},{24,16},{32,24},{40,32},{48,40},{56,48},{0,56},{9,1},... | collective-permute-start | bytes 368648 | tf_op jit(solution)/shard_map/ppermute | solution.py:514
  19.6 2.7 %collective-permute-done.4.low_c = f32[30,8,128]{2,1,0:T(8,128)S(1)} collective-permute-done((f32[30,8,128]{2,1,0:T(8,128)S(1)}, f32[30,8,128]{2,1,0:T(8,128)S(1)}, u32[]{:S(2)}, u32[]{:S(2)}) %collective-permute-start.4) | collective-permute-done | bytes 122912 | tf_op jit(solution)/shard_map/ppermute | solution.py:514
  22.3 0.0 collective-permute-done.5.high_c
  22.3 0.0 collective-permute-done.2.low_y
  22.3 0.0 collective-permute-done.3.high_y
  22.3 1.1 %to_lanes.1 = (f32[3,12,128,128]{3,2,1,0:T(8,128)S(1)}, f32[12,128,128]{2,1,0:T(8,128)S(1)}, f32[12,128,128]{2,1,0:T(8,128)S(1)}, f32[128,128]{1,0:T(8,128)S(1)}...) custom-call(f32[3,32,16,128]{3,2,1,0:T(8,128)S(1)} %get-tuple-element.28.force, ...), custom_call_target="tpu_custom_call" | custom-call | tf_op jit(solution)/shard_map/to_lanes/pallas_call | solution.py:495
  23.4 3.7 %collective-permute-start.6 = (f32[50,8,128]{2,1,0:T(8,128)S(1)}, f32[50,8,128]{2,1,0:T(8,128)S(1)}, u32[]{:S(2)}, u32[]{:S(2)}) collective-permute-start(f32[50,8,128]{2,1,0:T(8,128)S(1)} %get-tuple-element.38), channel_id=1, source_target_pairs={{0,1},{1,2},{2,3},{3,4},{4,5},{5,6},{6,7},{7,0},{8,9},{9,10},{10,1... | collective-permute-start | bytes 614408 | tf_op jit(solution)/shard_map/ppermute | solution.py:514
  27.2 0.0 collective-permute-start.7
  27.2 4.3 %prepare.1 = (f32[14,160,128]{2,1,0:T(8,128)S(1)}, f32[6,12,144,128]{3,2,1,0:T(8,128)S(1)}, f32[12,144,128]{2,1,0:T(8,128)S(1)}, f32[12,144,128]{2,1,0:T(8,128)S...) custom-call(f32[3,12,128,128]{3,2,1,0:T(8,128)S(1)} %get-tuple-element.36.f, ...), custom_call_target="tpu_custom_call" | custom-call | flops 23592960 | tf_op jit(solution)/shard_map/prepare/pallas_call | solution.py:495
  31.5 0.0 collective-permute-done.6.low_z
  31.5 0.8 %collective-permute-done.7.high_z = f32[50,8,128]{2,1,0:T(8,128)S(1)} collective-permute-done((f32[50,8,128]{2,1,0:T(8,128)S(1)}, f32[50,8,128]{2,1,0:T(8,128)S(1)}, u32[]{:S(2)}, u32[]{:S(2)}) %collective-permute-start.7) | collective-permute-done | bytes 204832 | tf_op jit(solution)/shard_map/ppermute | solution.py:514
  32.3 14.4 %solve_local.1 = (f32[14,160,128]{2,1,0:T(8,128)S(1)}, f32[6,12,144,128]{3,2,1,0:T(8,128)S(1)}, f32[12,144,128]{2,1,0:T(8,128)S(1)}, f32[12,144,128]{2,1,0:T(8,1...) custom-call(f32[3,12,128,128]{3,2,1,0:T(8,128)S(1)} %get-tuple-eleme, ...), custom_call_target="tpu_custom_call", output_to_operand_aliasing={{0}: (4, {}), {1}: (5, {}), {2}: (6, {}), {3}: (7, {}), {4}... | custom-call | tf_op jit(solution)/shard_map/solve_local/pallas_call | solution.py:495
  46.8 0.1 broadcast_in_dim.9
  46.8 24.1 %all_to_all.5 = f32[256,1,128]{2,1,0:T(1,128)S(1)} all-to-all(f32[256,1,128]{2,1,0:T(1,128)S(1)} %broadcast_in_dim.9), channel_id=1, replica_groups=mesh['gx'=4,'gy'=8,'gz'=8] {'gx','gy','gz'}, dimensions={0} | all-to-all | bytes 262144 | tf_op jit(solution)/shard_map/all_to_all | solution.py:556
  71.0 2.8 %combine.1 = (f32[4,32,16,128]{3,2,1,0:T(8,128)}, f32[4,32,16,128]{3,2,1,0:T(8,128)}) custom-call(f32[256,128]{1,0:T(8,128)S(1)} %bitcast.2, f32[3,12,128,128]{3,2,1,0:T(8,128)S(1)} %get-tuple-element.36.f, f32[3,12,128,128]{3,2,1,0:T(8,128)S(1)} %get-tuple-element.50.s0, f32[4,12,128,128]{3,2,1,0:T(8,128)S(1)} %get-tuple-element.51.u1, ...), custom_call_target="tpu_custom_call" | custom-call | tf_op jit(solution)/shard_map/combine/pallas_call | solution.py:495
  (1 shorter events, 0.0 us)
Async XLA Ops:
  1.9 20.3 %collective-permute-start.2 = (f32[132,8,128]{2,1,0:T(8,128)S(1)}, f32[132,8,128]{2,1,0:T(8,128)S(1)}, u32[]{:S(2)}, u32[]{:S(2)}) collective-permute-start(f32[132,8,128]{2,1,0:T(8,128)S(1)} %get-tuple-element.32), channel_id=1, source_target_pairs={{0,8},{8,16},{16,24},{24,32},{32,40},{40,48},{48,56},{56,0},{1,9},... | collective-permute-start | bytes 1622024 | tf_op jit(solution)/shard_map/ppermute | solution.py:514
  4.5 17.8 %collective-permute-start.3 = (f32[132,8,128]{2,1,0:T(8,128)S(1)}, f32[132,8,128]{2,1,0:T(8,128)S(1)}, u32[]{:S(2)}, u32[]{:S(2)}) collective-permute-start(f32[132,8,128]{2,1,0:T(8,128)S(1)} %get-tuple-element.33), channel_id=1, source_target_pairs={{8,0},{16,8},{24,16},{32,24},{40,32},{48,40},{56,48},{0,56},{9,1},... | collective-permute-start | bytes 1622024 | tf_op jit(solution)/shard_map/ppermute | solution.py:514
  8.5 8.3 %collective-permute-start = (f32[33,16,128]{2,1,0:T(8,128)S(1)}, f32[33,16,128]{2,1,0:T(8,128)S(1)}, u32[]{:S(2)}, u32[]{:S(2)}) collective-permute-start(f32[33,16,128]{2,1,0:T(8,128)S(1)} %get-tuple-element.30), channel_id=1, source_target_pairs={{0,64},{64,128},{128,192},{192,0},{1,65},{65,129},{129,193},{193,1... | collective-permute-start | bytes 811016 | tf_op jit(solution)/shard_map/ppermute | solution.py:514
  9.7 7.1 %collective-permute-start.1 = (f32[33,16,128]{2,1,0:T(8,128)S(1)}, f32[33,16,128]{2,1,0:T(8,128)S(1)}, u32[]{:S(2)}, u32[]{:S(2)}) collective-permute-start(f32[33,16,128]{2,1,0:T(8,128)S(1)} %get-tuple-element.31), channel_id=1, source_target_pairs={{64,0},{128,64},{192,128},{0,192},{65,1},{129,65},{193,129},{1,193... | collective-permute-start | bytes 811016 | tf_op jit(solution)/shard_map/ppermute | solution.py:514
  16.9 5.4 %collective-permute-start.4 = (f32[30,8,128]{2,1,0:T(8,128)S(1)}, f32[30,8,128]{2,1,0:T(8,128)S(1)}, u32[]{:S(2)}, u32[]{:S(2)}) collective-permute-start(f32[30,8,128]{2,1,0:T(8,128)S(1)} %get-tuple-element.34), channel_id=1, source_target_pairs={{0,8},{8,16},{16,24},{24,32},{32,40},{40,48},{48,56},{56,0},{1,9},... | collective-permute-start | bytes 368648 | tf_op jit(solution)/shard_map/ppermute | solution.py:514
  16.9 5.3 %collective-permute-start.5 = (f32[30,8,128]{2,1,0:T(8,128)S(1)}, f32[30,8,128]{2,1,0:T(8,128)S(1)}, u32[]{:S(2)}, u32[]{:S(2)}) collective-permute-start(f32[30,8,128]{2,1,0:T(8,128)S(1)} %get-tuple-element.35), channel_id=1, source_target_pairs={{8,0},{16,8},{24,16},{32,24},{40,32},{48,40},{56,48},{0,56},{9,1},... | collective-permute-start | bytes 368648 | tf_op jit(solution)/shard_map/ppermute | solution.py:514
  23.4 8.1 %collective-permute-start.6 = (f32[50,8,128]{2,1,0:T(8,128)S(1)}, f32[50,8,128]{2,1,0:T(8,128)S(1)}, u32[]{:S(2)}, u32[]{:S(2)}) collective-permute-start(f32[50,8,128]{2,1,0:T(8,128)S(1)} %get-tuple-element.38), channel_id=1, source_target_pairs={{0,1},{1,2},{2,3},{3,4},{4,5},{5,6},{6,7},{7,0},{8,9},{9,10},{10,1... | collective-permute-start | bytes 614408 | tf_op jit(solution)/shard_map/ppermute | solution.py:514
  27.2 5.2 %collective-permute-start.7 = (f32[50,8,128]{2,1,0:T(8,128)S(1)}, f32[50,8,128]{2,1,0:T(8,128)S(1)}, u32[]{:S(2)}, u32[]{:S(2)}) collective-permute-start(f32[50,8,128]{2,1,0:T(8,128)S(1)} %get-tuple-element.39), channel_id=1, source_target_pairs={{1,0},{2,1},{3,2},{4,3},{5,4},{6,5},{7,6},{0,7},{9,8},{10,9},{11,1... | collective-permute-start | bytes 614408 | tf_op jit(solution)/shard_map/ppermute | solution.py:514

commit v5 on v4

--- a/solution.py
+++ b/solution.py
@@ -1,11 +1,10 @@
-import functools
-
 import jax
 import jax.numpy as jnp
 from jax import lax
 from jax.experimental import pallas as pl
 from jax.experimental.pallas import tpu as pltpu
 from jax.sharding import PartitionSpec as P
+
 
 CHEB = 4
 LOW_EDGE = 0.25
@@ -94,7 +93,12 @@
     return lax.axis_index(axis) == lax.axis_size(axis) - 1
 
 
-def pack_faces(force_in, visc_in, force, visc, tail_x, head_x, tail_y, head_y, arrived):
+def at_even(axis):
+    return lax.axis_index(axis) % 2 == 0
+
+
+def pack_faces(force_in, visc_in, force, visc, tail_x, head_x, first_y, second_y, arrived):
+    even = at_even("gy")
     copies = [
         pltpu.make_async_copy(visc_in, visc, arrived.at[0]),
         pltpu.make_async_copy(force_in, force, arrived.at[1]),
@@ -104,16 +108,22 @@
     copies[0].wait()
     tail_x[24:] = visc[BX - 9 :]
     head_x[24:] = visc[:9]
-    for out, first, ninth in ((tail_y, BY - 8, BY - 9), (head_y, 0, 8)):
-        out[3 * BX : 4 * BX] = visc[:, first : first + 8, :]
+    top, bottom = (BY - 8, BY - 9), (0, 8)
+    starts = [
+        [jnp.where(even, one, two) for one, two in zip(near, far)]
+        for near, far in ((top, bottom), (bottom, top))
+    ]
+    for out, (first, ninth) in zip((first_y, second_y), starts):
+        rows = pl.ds(pl.multiple_of(first, 8), 8)
+        out[3 * BX : 4 * BX] = visc[:, rows, :]
         for x in range(BX):
-            out[4 * BX + x // 8, x % 8 : x % 8 + 1, :] = visc[x, ninth : ninth + 1, :]
+            out[4 * BX + x // 8, x % 8 : x % 8 + 1, :] = visc[x, pl.ds(ninth, 1), :]
     copies[1].wait()
     for c in range(3):
         tail_x[c * 8 : c * 8 + 8] = force[c, BX - 8 :]
         head_x[c * 8 : c * 8 + 8] = force[c, :8]
-        tail_y[c * BX : c * BX + BX] = force[c, :, BY - 8 :, :]
-        head_y[c * BX : c * BX + BX] = force[c, :, :8, :]
+        for out, (first, _) in zip((first_y, second_y), starts):
+            out[c * BX : c * BX + BX] = force[c, :, pl.ds(pl.multiple_of(first, 8), 8), :]
 
 
 def pack_corners(low_x, high_x, tail, head):
@@ -144,12 +154,17 @@
 
 
 def to_lanes(
-    force, visc, low_x, high_x, low_y, high_y, low_c, high_c,
+    force, visc, low_x, high_x, first_y, second_y, low_c, high_c,
     f_out, v_out, ry_out, ex_out, tail, head,
 ):
     x_below, x_above = ~at_start("gx"), ~at_end("gx")
     y_below, y_above = ~at_start("gy"), ~at_end("gy")
     places = [corner_places(c) for c in range(4)]
+    even = at_even("gy")
+
+    def beside(*at):
+        one, two = first_y[at], second_y[at]
+        return jnp.where(even, two, one), jnp.where(even, one, two)
 
     def rows_of(c, at):
         x = at - H
@@ -160,7 +175,7 @@
         else:
             middle = force[c, x] if c < 3 else visc[x]
         if 0 <= x < BX:
-            lower, upper = low_y[c * BX + x], high_y[c * BX + x]
+            lower, upper = beside(c * BX + x)
         elif at in places[c]:
             where, count, second = places[c][at]
             lower, upper = low_c[where], high_c[where]
@@ -195,8 +210,8 @@
             x = k * SLABS + g - H
             if 0 <= x < BX:
                 at = 4 * BX + x // 8
-                lower = kept_if(y_below, low_y[at, x % 8 : x % 8 + 1, :])
-                upper = kept_if(y_above, high_y[at, x % 8 : x % 8 + 1, :])
+                lower, upper = beside(at, slice(x % 8, x % 8 + 1))
+                lower, upper = kept_if(y_below, lower), kept_if(y_above, upper)
             else:
                 lower = upper = jnp.zeros((1, BZ), jnp.float32)
             parts += [lower, nothing, upper]
@@ -486,7 +501,7 @@
 
 
 def call(
-    kernel, outs, scratch=(), name=None, mib=16, source=pltpu.VMEM, to=pltpu.VMEM, alias=None, flops=None
+    kernel, outs, scratch=(), mib=16, source=pltpu.VMEM, to=pltpu.VMEM, alias=None, flops=None
 ):
     result = pl.BlockSpec(memory_space=to)
     given = pl.BlockSpec(memory_space=source)
@@ -501,7 +516,6 @@
             cost_estimate=flops and pl.CostEstimate(flops=flops, bytes_accessed=0, transcendentals=0),
             scratch_shapes=list(scratch),
             compiler_params=pltpu.CompilerParams(vmem_limit_bytes=mib * 1024 * 1024),
-            name=name,
         )(*args)
 
     return run
@@ -511,44 +525,51 @@
     count = lax.axis_size(axis)
     up = [(i, (i + 1) % count) for i in range(count)]
     down = [(j, i) for i, j in up]
-    return lax.ppermute(tail, axis, up), lax.ppermute(head, axis, down)
+    low = lax.ppermute(tail, axis, up)
+    high = lax.ppermute(head, axis, down)
+    return low, high
+
+
+def swap_pairs(first, second, axis):
+    count = lax.axis_size(axis)
+    pairs = [[], []]
+    for i in range(count):
+        pairs[i % 2] += [(i, (i + 1) % count), ((i + 1) % count, i)]
+    first = lax.ppermute(first, axis, pairs[0])
+    second = lax.ppermute(second, axis, pairs[1])
+    return first, second
 
 
 def shards(viscosity, force):
-    force, viscosity, tail_x, head_x, tail_y, head_y = call(
+    force, viscosity, tail_x, head_x, first_y, second_y = call(
         pack_faces,
         [kept(3, BX, BY, BZ), kept(BX, BY, BZ)]
         + [kept(33, BY, BZ)] * 2
         + [kept(FACE_TILES, 8, BZ)] * 2,
         [pltpu.SemaphoreType.DMA((2,))],
-        name="pack_faces",
         source=pltpu.HBM,
     )(*(pltpu.with_memory_space_constraint(x, pltpu.HBM) for x in (force, viscosity)))
-    low_y, high_y = swap(tail_y, head_y, "gy")
+    first_y, second_y = swap_pairs(first_y, second_y, "gy")
     low_x, high_x = swap(tail_x, head_x, "gx")
-    tail, head = call(pack_corners, [kept(CORNER_TILES, 8, BZ)] * 2, name="pack_corners")(
-        low_x, high_x
-    )
+    tail, head = call(pack_corners, [kept(CORNER_TILES, 8, BZ)] * 2)(low_x, high_x)
     low_c, high_c = swap(tail, head, "gy")
     field = (SLABS, BZ, LANES)
     f, v, ry, ex, tail, head = call(
         to_lanes,
         [kept(3, *field), kept(*field), kept(*field), kept(BZ, LANES)]
         + [kept(ZTILES, 8, LANES)] * 2,
-        name="to_lanes",
-    )(force, viscosity, low_x, high_x, low_y, high_y, low_c, high_c)
+    )(force, viscosity, low_x, high_x, first_y, second_y, low_c, high_c)
     low_z, high_z = swap(tail, head, "gz")
     ghosted = (SLABS + 2, ROWS, LANES)
     plain = (SLABS, EZ, LANES)
     state_shapes = [kept(*ghosted), kept(6, *plain), kept(*plain), kept(*plain)]
     state_shapes += [kept(3, *ghosted)] * 3
-    state = call(prepare, state_shapes, name="prepare", flops=120 * EX * EY * BZ)(f, v, ry, ex)
+    state = call(prepare, state_shapes, flops=120 * EX * EY * BZ)(f, v, ry, ex)
     *_, s0, u1, s1, u2, sums = call(
         solve_local,
         state_shapes
         + [kept(3, *field), kept(4, *field), kept(4, *field), kept(4, *field), kept(1, LANES)],
         [pltpu.VMEM((3, *ghosted), jnp.float32), pltpu.VMEM(ghosted, jnp.float32)],
-        name="solve_local",
         alias={4 + i: i for i in range(7)},
     )(f, ry, low_z, high_z, *state)
     devices = lax.axis_size(AXES)
@@ -558,11 +579,7 @@
     whole = pltpu.VMEM((4, BX, BY, BZ), jnp.float32)
     return tuple(
         call(
-            combine,
-            [block, block],
-            [whole, whole, pltpu.SemaphoreType.DMA((8,))],
-            name="combine",
-            to=pltpu.HBM,
+            combine, [block, block], [whole, whole, pltpu.SemaphoreType.DMA((8,))], to=pltpu.HBM
         )(gathered, f, s0, u1, s1, u2)
     )
 

time: 74 us -> 73.9 us (level)
  blocking collectives: 24.1 us -> 23.3 us
    all_to_all x1, blocking collectives: 24.1 us -> 23.3 us  [shards(): gathered = lax.all_to_all(rows, AXES, 0, 0).reshape(devices, LANES)]
where the time goes in v5:
time: 73.9 us; the launch traced here: 73.7 us
  Pallas kernels  24 us (32%)
  blocking collectives  23.3 us (32%)
  starting transfers between devices  16.3 us (22%)
  waiting for transfers between devices  9.2 us (12%)
  between operations  0.87 us (1%)
    pallas_call x6, Pallas kernels, run(): pl.pallas_call(kernel, out_shape=outs, in_specs=[given] * len(args), out_...  24 us
    all_to_all x1, blocking collectives, shards(): gathered = lax.all_to_all(rows, AXES, 0, 0).reshape(devices, LANES)  23.3 us
    ppermute x3, waiting for transfers between devices, swap(): low = lax.ppermute(tail, axis, up)  8.38 us
    ppermute x3, starting transfers between devices, swap(): low = lax.ppermute(tail, axis, up)  4.95 us
    ppermute x1, starting transfers between devices, swap_pairs(): second = lax.ppermute(second, axis, pairs[1])  4.67 us
    ppermute x3, starting transfers between devices, swap(): high = lax.ppermute(head, axis, down)  4.13 us
    ppermute x1, starting transfers between devices, swap_pairs(): first = lax.ppermute(first, axis, pairs[0])  2.54 us
  transfers between devices with their start and end apart: 8, of which 3 were waited for; matrix products, arithmetic and copies ran while one was open for 0% of the time, Pallas kernels for 6%

profile of v5, /device:TPU:1, one launch (start us, length us, event | category | flops | bytes accessed | tf_op | source)
XLA Modules:
  0.0 73.7 jit_solution(14954059644895585910)
XLA Ops:
  0.6 1.3 %shard_map.41 = (f32[3,32,16,128]{3,2,1,0:T(8,128)S(1)}, f32[32,16,128]{2,1,0:T(8,128)S(1)}, f32[33,16,128]{2,1,0:T(8,128)S(1)}, f32[33,16,128]{2,1,0:T(8,128)S(...) custom-call(f32[3,32,16,128]{3,2,1,0:T(8,128)} %force_in.1, f32[32,16,128]{2,1,0:T(8,128)} %visc_in.1), custom_call_target="tpu_custom_call" | custom-call | tf_op jit(solution)/shard_map/pallas_call | solution.py:510
  1.9 2.5 %collective-permute-start.2 = (f32[132,8,128]{2,1,0:T(8,128)S(1)}, f32[132,8,128]{2,1,0:T(8,128)S(1)}, u32[]{:S(2)}, u32[]{:S(2)}) collective-permute-start(f32[132,8,128]{2,1,0:T(8,128)S(1)} %get-tuple-element.32), channel_id=1, source_target_pairs={{0,8},{8,0},{16,24},{24,16},{32,40},{40,32},{48,56},{56,48},{1,9},... | collective-permute-start | bytes 1622024 | tf_op jit(solution)/shard_map/ppermute | solution.py:538
  4.5 4.7 %collective-permute-start.3 = (f32[132,8,128]{2,1,0:T(8,128)S(1)}, f32[132,8,128]{2,1,0:T(8,128)S(1)}, u32[]{:S(2)}, u32[]{:S(2)}) collective-permute-start(f32[132,8,128]{2,1,0:T(8,128)S(1)} %get-tuple-element.33), channel_id=1, source_target_pairs={{8,16},{16,8},{24,32},{32,24},{40,48},{48,40},{56,0},{0,56},{9,17}... | collective-permute-start | bytes 1622024 | tf_op jit(solution)/shard_map/ppermute | solution.py:539
  9.2 1.2 %collective-permute-start = (f32[33,16,128]{2,1,0:T(8,128)S(1)}, f32[33,16,128]{2,1,0:T(8,128)S(1)}, u32[]{:S(2)}, u32[]{:S(2)}) collective-permute-start(f32[33,16,128]{2,1,0:T(8,128)S(1)} %get-tuple-element.30), channel_id=1, source_target_pairs={{0,64},{64,128},{128,192},{192,0},{1,65},{65,129},{129,193},{193,1... | collective-permute-start | bytes 811016 | tf_op jit(solution)/shard_map/ppermute | solution.py:528
  10.4 1.5 %collective-permute-start.1 = (f32[33,16,128]{2,1,0:T(8,128)S(1)}, f32[33,16,128]{2,1,0:T(8,128)S(1)}, u32[]{:S(2)}, u32[]{:S(2)}) collective-permute-start(f32[33,16,128]{2,1,0:T(8,128)S(1)} %get-tuple-element.31), channel_id=1, source_target_pairs={{64,0},{128,64},{192,128},{0,192},{65,1},{129,65},{193,129},{1,193... | collective-permute-start | bytes 811016 | tf_op jit(solution)/shard_map/ppermute | solution.py:529
  11.8 5.3 %collective-permute-done.low_x = f32[33,16,128]{2,1,0:T(8,128)S(1)} collective-permute-done((f32[33,16,128]{2,1,0:T(8,128)S(1)}, f32[33,16,128]{2,1,0:T(8,128)S(1)}, u32[]{:S(2)}, u32[]{:S(2)}) %collective-permute-start) | collective-permute-done | bytes 270368 | tf_op jit(solution)/shard_map/ppermute | solution.py:528
  17.2 0.0 collective-permute-done.1.high_x
  17.2 0.1 collective-permute-start.4
  17.3 2.7 %collective-permute-start.5 = (f32[30,8,128]{2,1,0:T(8,128)S(1)}, f32[30,8,128]{2,1,0:T(8,128)S(1)}, u32[]{:S(2)}, u32[]{:S(2)}) collective-permute-start(f32[30,8,128]{2,1,0:T(8,128)S(1)} %get-tuple-element.35), channel_id=1, source_target_pairs={{8,0},{16,8},{24,16},{32,24},{40,32},{48,40},{56,48},{0,56},{9,1},... | collective-permute-start | bytes 368648 | tf_op jit(solution)/shard_map/ppermute | solution.py:529
  20.0 3.0 %collective-permute-done.4.low_c = f32[30,8,128]{2,1,0:T(8,128)S(1)} collective-permute-done((f32[30,8,128]{2,1,0:T(8,128)S(1)}, f32[30,8,128]{2,1,0:T(8,128)S(1)}, u32[]{:S(2)}, u32[]{:S(2)}) %collective-permute-start.4) | collective-permute-done | bytes 122912 | tf_op jit(solution)/shard_map/ppermute | solution.py:528
  23.0 0.0 collective-permute-done.5.high_c
  23.0 0.0 collective-permute-done.2.first_y
  23.0 0.0 collective-permute-done.3.second_y
  23.0 1.1 %shard_map.43 = (f32[3,12,128,128]{3,2,1,0:T(8,128)S(1)}, f32[12,128,128]{2,1,0:T(8,128)S(1)}, f32[12,128,128]{2,1,0:T(8,128)S(1)}, f32[128,128]{1,0:T(8,128)S(1...) custom-call(f32[3,32,16,128]{3,2,1,0:T(8,128)S(1)} %get-tuple-element.28.force, ...), custom_call_target="tpu_custom_call" | custom-call | tf_op jit(solution)/shard_map/pallas_call | solution.py:510
  24.2 3.7 %collective-permute-start.6 = (f32[50,8,128]{2,1,0:T(8,128)S(1)}, f32[50,8,128]{2,1,0:T(8,128)S(1)}, u32[]{:S(2)}, u32[]{:S(2)}) collective-permute-start(f32[50,8,128]{2,1,0:T(8,128)S(1)} %get-tuple-element.38), channel_id=1, source_target_pairs={{0,1},{1,2},{2,3},{3,4},{4,5},{5,6},{6,7},{7,0},{8,9},{9,10},{10,1... | collective-permute-start | bytes 614408 | tf_op jit(solution)/shard_map/ppermute | solution.py:528
  27.8 0.0 collective-permute-start.7
  27.8 4.3 %shard_map.44 = (f32[14,160,128]{2,1,0:T(8,128)S(1)}, f32[6,12,144,128]{3,2,1,0:T(8,128)S(1)}, f32[12,144,128]{2,1,0:T(8,128)S(1)}, f32[12,144,128]{2,1,0:T(8,12...) custom-call(f32[3,12,128,128]{3,2,1,0:T(8,128)S(1)} %get-tuple-element.36., ...), custom_call_target="tpu_custom_call" | custom-call | flops 23592960 | tf_op jit(solution)/shard_map/pallas_call | solution.py:510
  32.2 0.0 collective-permute-done.6.low_z
  32.2 0.8 %collective-permute-done.7.high_z = f32[50,8,128]{2,1,0:T(8,128)S(1)} collective-permute-done((f32[50,8,128]{2,1,0:T(8,128)S(1)}, f32[50,8,128]{2,1,0:T(8,128)S(1)}, u32[]{:S(2)}, u32[]{:S(2)}) %collective-permute-start.7) | collective-permute-done | bytes 204832 | tf_op jit(solution)/shard_map/ppermute | solution.py:529
  33.0 14.4 %shard_map.45 = (f32[14,160,128]{2,1,0:T(8,128)S(1)}, f32[6,12,144,128]{3,2,1,0:T(8,128)S(1)}, f32[12,144,128]{2,1,0:T(8,128)S(1)}, f32[12,144,128]{2,1,0:T(8,12...) custom-call(f32[3,12,128,128]{3,2,1,0:T(8,128)S(1)} %get-tuple-eleme, ...), custom_call_target="tpu_custom_call", output_to_operand_aliasing={{0}: (4, {}), {1}: (5, {}), {2}: (6, {}), {3}: (7, {}), {4}... | custom-call | tf_op jit(solution)/shard_map/pallas_call | solution.py:510
  47.4 0.1 broadcast_in_dim.9
  47.5 23.3 %all_to_all.5 = f32[256,1,128]{2,1,0:T(1,128)S(1)} all-to-all(f32[256,1,128]{2,1,0:T(1,128)S(1)} %broadcast_in_dim.9), channel_id=1, replica_groups=mesh['gx'=4,'gy'=8,'gz'=8] {'gx','gy','gz'}, dimensions={0} | all-to-all | bytes 262144 | tf_op jit(solution)/shard_map/all_to_all | solution.py:577
  70.8 2.8 %shard_map.46 = (f32[4,32,16,128]{3,2,1,0:T(8,128)}, f32[4,32,16,128]{3,2,1,0:T(8,128)}) custom-call(f32[256,128]{1,0:T(8,128)S(1)} %bitcast.2, f32[3,12,128,128]{3,2,1,0:T(8,128)S(1)} %get-tuple-element.36.f, f32[3,12,128,128]{3,2,1,0:T(8,128)S(1)} %get-tuple-element.50.s0, f32[4,12,128,128]{3,2,1,0:T(8,128)S(1)} %get-tuple-element.51.u1, ...), custom_call_target="tpu_custom_call" | custom-call | tf_op jit(solution)/shard_map/pallas_call | solution.py:510
  (1 shorter events, 0.0 us)
Async XLA Ops:
  1.9 21.1 %collective-permute-start.2 = (f32[132,8,128]{2,1,0:T(8,128)S(1)}, f32[132,8,128]{2,1,0:T(8,128)S(1)}, u32[]{:S(2)}, u32[]{:S(2)}) collective-permute-start(f32[132,8,128]{2,1,0:T(8,128)S(1)} %get-tuple-element.32), channel_id=1, source_target_pairs={{0,8},{8,0},{16,24},{24,16},{32,40},{40,32},{48,56},{56,48},{1,9},... | collective-permute-start | bytes 1622024 | tf_op jit(solution)/shard_map/ppermute | solution.py:538
  4.5 18.5 %collective-permute-start.3 = (f32[132,8,128]{2,1,0:T(8,128)S(1)}, f32[132,8,128]{2,1,0:T(8,128)S(1)}, u32[]{:S(2)}, u32[]{:S(2)}) collective-permute-start(f32[132,8,128]{2,1,0:T(8,128)S(1)} %get-tuple-element.33), channel_id=1, source_target_pairs={{8,16},{16,8},{24,32},{32,24},{40,48},{48,40},{56,0},{0,56},{9,17}... | collective-permute-start | bytes 1622024 | tf_op jit(solution)/shard_map/ppermute | solution.py:539
  9.2 8.0 %collective-permute-start = (f32[33,16,128]{2,1,0:T(8,128)S(1)}, f32[33,16,128]{2,1,0:T(8,128)S(1)}, u32[]{:S(2)}, u32[]{:S(2)}) collective-permute-start(f32[33,16,128]{2,1,0:T(8,128)S(1)} %get-tuple-element.30), channel_id=1, source_target_pairs={{0,64},{64,128},{128,192},{192,0},{1,65},{65,129},{129,193},{193,1... | collective-permute-start | bytes 811016 | tf_op jit(solution)/shard_map/ppermute | solution.py:528
  10.4 6.8 %collective-permute-start.1 = (f32[33,16,128]{2,1,0:T(8,128)S(1)}, f32[33,16,128]{2,1,0:T(8,128)S(1)}, u32[]{:S(2)}, u32[]{:S(2)}) collective-permute-start(f32[33,16,128]{2,1,0:T(8,128)S(1)} %get-tuple-element.31), channel_id=1, source_target_pairs={{64,0},{128,64},{192,128},{0,192},{65,1},{129,65},{193,129},{1,193... | collective-permute-start | bytes 811016 | tf_op jit(solution)/shard_map/ppermute | solution.py:529
  17.2 5.8 %collective-permute-start.4 = (f32[30,8,128]{2,1,0:T(8,128)S(1)}, f32[30,8,128]{2,1,0:T(8,128)S(1)}, u32[]{:S(2)}, u32[]{:S(2)}) collective-permute-start(f32[30,8,128]{2,1,0:T(8,128)S(1)} %get-tuple-element.34), channel_id=1, source_target_pairs={{0,8},{8,16},{16,24},{24,32},{32,40},{40,48},{48,56},{56,0},{1,9},... | collective-permute-start | bytes 368648 | tf_op jit(solution)/shard_map/ppermute | solution.py:528
  17.3 5.7 %collective-permute-start.5 = (f32[30,8,128]{2,1,0:T(8,128)S(1)}, f32[30,8,128]{2,1,0:T(8,128)S(1)}, u32[]{:S(2)}, u32[]{:S(2)}) collective-permute-start(f32[30,8,128]{2,1,0:T(8,128)S(1)} %get-tuple-element.35), channel_id=1, source_target_pairs={{8,0},{16,8},{24,16},{32,24},{40,32},{48,40},{56,48},{0,56},{9,1},... | collective-permute-start | bytes 368648 | tf_op jit(solution)/shard_map/ppermute | solution.py:529
  24.2 8.0 %collective-permute-start.6 = (f32[50,8,128]{2,1,0:T(8,128)S(1)}, f32[50,8,128]{2,1,0:T(8,128)S(1)}, u32[]{:S(2)}, u32[]{:S(2)}) collective-permute-start(f32[50,8,128]{2,1,0:T(8,128)S(1)} %get-tuple-element.38), channel_id=1, source_target_pairs={{0,1},{1,2},{2,3},{3,4},{4,5},{5,6},{6,7},{7,0},{8,9},{9,10},{10,1... | collective-permute-start | bytes 614408 | tf_op jit(solution)/shard_map/ppermute | solution.py:528
  27.8 5.2 %collective-permute-start.7 = (f32[50,8,128]{2,1,0:T(8,128)S(1)}, f32[50,8,128]{2,1,0:T(8,128)S(1)}, u32[]{:S(2)}, u32[]{:S(2)}) collective-permute-start(f32[50,8,128]{2,1,0:T(8,128)S(1)} %get-tuple-element.39), channel_id=1, source_target_pairs={{1,0},{2,1},{3,2},{4,3},{5,4},{6,5},{7,6},{0,7},{9,8},{10,9},{11,1... | collective-permute-start | bytes 614408 | tf_op jit(solution)/shard_map/ppermute | solution.py:529
